TPU v7x, 256 devices: a whole 4x4x8 slice. The times are simulated.
256 devices in a mesh: img: 4 (over y_hi, core), txt: 64 (over x, y_lo, z).
Axes of the slice: x: 4, y: 4 (y_hi: 2, y_lo: 2; y = y_hi * 2 + y_lo), z: 8, core: 2. Of those that a mesh axis runs over, the one named last changes fastest.
Arguments:
- queries: bfloat16 [1, 40960, 8192], P(None, 'txt', 'img'), may hold values from -128 to 128
- visual_keys: bfloat16 [1, 512, 8192], P(None, 'img'), may hold values from -5 to 5
- visual_values: bfloat16 [1, 512, 8192], P(None, 'img'), may hold values from -6 to 6
- out_grad: bfloat16 [1, 40960, 8192], P(None, 'txt', 'img'), may hold values from -6 to 6
- gate_value: float32 [1, 64], P(None, 'img'), may hold values from -1.5 to 1.5
- image_order: int32 [1, 8], replicated, may hold values from 0 to 7, as said below
- image_seen: int32 [40960], P('txt'), may hold values from 1 to 8
Outputs:
- query_grad: bfloat16 [1, 40960, 8192], P(None, 'txt', 'img')
- key_grad: float32 [1, 512, 8192], P(None, 'txt', 'img')
- value_grad: float32 [1, 512, 8192], P(None, 'txt', 'img')
Inputs may be any that keep to these rules, and one draw needn't show every extreme that they name: `image_order`: each row names every image of 0 to 7 once.
All inputs are finite; a program needn't handle non-finite values.
Results may differ from a plain program's by a relative error of at most 0.0058.
Values may be sent and summed in bfloat16 or wider, within the bound.
No kernel may reach another device: no remote copies, remote signals or barrier semaphores. Data moves between devices by JAX's collectives and lax.ppermute only.
A program may use at most 128 MiB of HBM per device.

v0:
```python
import math

import jax
import jax.numpy as jnp
from jax import lax
from jax.sharding import PartitionSpec as P


def cut_along(shard, dim, peers):
    before, after = (shard.shape[:dim], shard.shape[dim + 1 :])
    return jnp.moveaxis(shard.reshape(*before, peers, -1, *after), dim, 0)


def summed_on_arrival(shard, axis, dim):
    blocks = cut_along(shard, dim, lax.axis_size(axis))
    arrived = lax.all_to_all(blocks, axis, split_axis=0, concat_axis=0, tiled=True)
    return arrived.astype(jnp.float32).sum(axis=0)


def in_one_piece(arrays, axis, dim, along):
    both = jnp.concatenate(arrays, axis=along)
    result, at, finished = (summed_on_arrival(both, axis, dim), 0, [])
    for a in arrays:
        finished.append(lax.slice_in_dim(result, at, at + a.shape[along], axis=along))
        at += a.shape[along]
    return tuple(finished)


def image_mask(order_row, image_seen, key_count):
    image_count = order_row.shape[0]
    latent_count = key_count // image_count
    key_image = jnp.broadcast_to(order_row[:, None], (image_count, latent_count)).reshape(key_count)
    return key_image[None, :] < image_seen[:, None]


def attention_grads(query, grad_in, factor, key_rows, value_rows, allowed, score_scale):
    token_count = query.shape[0]
    head_count = factor.shape[0]
    head_width = query.shape[1] // head_count
    key_count = key_rows.shape[0]
    query_heads = query.reshape(token_count, head_count, head_width)
    key_heads = key_rows.reshape(key_count, head_count, head_width)
    value_heads = value_rows.reshape(key_count, head_count, head_width)
    gated_grad = (
        grad_in.reshape(token_count, head_count, head_width).astype(jnp.float32)
        * factor[None, :, None]
    ).astype(jnp.bfloat16)
    scores = (
        jnp.einsum("thd,khd->htk", query_heads, key_heads, preferred_element_type=jnp.float32)
        * score_scale
    )
    masked = jnp.where(allowed[None], scores, -1e30)
    row_max = jnp.max(masked, axis=2, keepdims=True)
    exponent = jnp.where(allowed[None], jnp.exp(masked - row_max), 0.0)
    weights = exponent / jnp.sum(exponent, axis=2, keepdims=True)
    weight_half = weights.astype(jnp.bfloat16)
    attended = jnp.einsum(
        "htk,khd->thd", weight_half, value_heads, preferred_element_type=jnp.float32
    )
    row_delta = jnp.sum(gated_grad.astype(jnp.float32) * attended, axis=2)
    weight_grad = jnp.einsum(
        "thd,khd->htk", gated_grad, value_heads, preferred_element_type=jnp.float32
    )
    score_half = (weights * (weight_grad - jnp.transpose(row_delta)[:, :, None])).astype(
        jnp.bfloat16
    )
    query_part = (
        jnp.einsum("htk,khd->thd", score_half, key_heads, preferred_element_type=jnp.float32)
        * score_scale
    )
    return (
        query_part.astype(jnp.bfloat16).reshape(token_count, -1),
        score_half,
        weight_half,
        query_heads,
        gated_grad,
    )


def latent_terms(score_half, weight_half, query_heads, gated_grad, count, score_scale):
    key_part = (
        jnp.einsum("htk,thd->khd", score_half, query_heads, preferred_element_type=jnp.float32)
        * score_scale
    )
    value_part = jnp.einsum(
        "htk,thd->khd", weight_half, gated_grad, preferred_element_type=jnp.float32
    )
    return (key_part.reshape(count, -1), value_part.reshape(count, -1))


def shards(queries, visual_keys, visual_values, out_grad, gate_value, image_order, image_seen):
    width_local = queries.shape[2]
    head_width = width_local // gate_value.shape[1]
    score_scale = 1.0 / math.sqrt(head_width)
    key_rows = lax.all_to_all(visual_keys[0], "img", split_axis=1, concat_axis=0, tiled=True)
    value_rows = lax.all_to_all(visual_values[0], "img", split_axis=1, concat_axis=0, tiled=True)
    key_total = key_rows.shape[0]
    allowed = image_mask(image_order[0], image_seen, key_total)
    factor = jnp.tanh(gate_value[0])
    query_part, score_half, weight_half, query_heads, gated_grad = attention_grads(
        queries[0], out_grad[0], factor, key_rows, value_rows, allowed, score_scale
    )
    query_list = [query_part]
    key_part, value_part = latent_terms(
        score_half, weight_half, query_heads, gated_grad, key_total, score_scale
    )
    key_share, value_share = in_one_piece(
        (key_part.astype(jnp.bfloat16), value_part.astype(jnp.bfloat16)), "txt", 0, 1
    )
    key_list = [key_share]
    value_list = [value_share]
    key_grad = jnp.stack(key_list)
    value_grad = jnp.stack(value_list)
    return (jnp.stack(query_list), key_grad, value_grad)


def solution(mesh):
    placed = (
        P(None, "txt", "img"),
        P(None, "img", None),
        P(None, "img", None),
        P(None, "txt", "img"),
        P(None, "img"),
        P(),
        P("txt"),
    )
    return jax.shard_map(
        shards,
        mesh=mesh,
        in_specs=placed,
        out_specs=(P(None, "txt", "img"), P(None, "txt", "img"), P(None, "txt", "img")),
        check_vma=False,
    )
```

profile of v0, /device:TPU:2, one launch (start us, length us, event | category | flops | bytes accessed | tf_op | source)
XLA Modules:
  0.0 285.8 jit_solution(16032215586573750900)
XLA Ops:
  6.4 4.5 %all-to-all-start = ((bf16[128,4,2048]{2,0,1:T(8,128)(2,1)}), bf16[128,4,2048]{2,0,1:T(8,128)(2,1)S(1)}, u32[]{:S(2)}, u32[]{:S(2)}) async-start(bf16[128,4,2048]{2,0,1:T(8,128)(2,1)} %copy.21), calls=%async_computation | async-start | bytes 4194304 | tf_op jit(solution)/shard_map/all_to_all | solution.py:95
  10.9 4.5 %all_to_all.30 = bf16[128,4,2048]{2,1,0:T(4,128)(2,1)} reshape(bf16[1,128,8192]{2,1,0:T(8,128)(2,1)} %param.9) | data formatting | bytes 4194304 | tf_op jit(solution)/shard_map/all_to_all | solution.py:96
  15.4 4.1 %copy.25 = bf16[128,4,2048]{2,0,1:T(8,128)(2,1)} copy(bf16[128,4,2048]{2,1,0:T(4,128)(2,1)} %all_to_all.30) | data formatting | bytes 4194304 | tf_op jit(solution)/shard_map/all_to_all | solution.py:96
  19.5 18.6 %all-to-all-done = bf16[128,4,2048]{2,0,1:T(8,128)(2,1)S(1)} async-done(((bf16[128,4,2048]{2,0,1:T(8,128)(2,1)}), bf16[128,4,2048]{2,0,1:T(8,128)(2,1)S(1)}, u32[]{:S(2)}, u32[]{:S(2)}) %all-to-all-start) | async-done | bytes 2097184 | tf_op jit(solution)/shard_map/all_to_all | solution.py:95
  38.1 4.6 %all-to-all-start.1 = ((bf16[128,4,2048]{2,0,1:T(8,128)(2,1)}), bf16[128,4,2048]{2,0,1:T(8,128)(2,1)}, u32[]{:S(2)}, u32[]{:S(2)}) async-start(bf16[128,4,2048]{2,0,1:T(8,128)(2,1)} %copy.25), calls=%async_computation.1 | async-start | bytes 4194304 | tf_op jit(solution)/shard_map/all_to_all | solution.py:96
  47.0 4.9 %copy.24 = f32[1,640,2048]{1,2,0:T(8,128)} copy(bf16[1,640,2048]{2,1,0:T(8,128)(2,1)} %param.10) | data formatting | bytes 7864320 | tf_op jit(solution)/shard_map/convert_element_type | solution.py:45
  52.1 4.6 %multiply_convert_fusion.2 = bf16[640,16,128]{0,2,1:T(8,128)(2,1)} fusion(f32[640,16,128]{0,2,1:T(8,128)} %bitcast.41, f32[16]{0:T(128)S(1)} %tanh_bitcast_fusion), kind=kLoop, calls=%fused_computation.14 | loop fusion | flops 2621440 | bytes 7864384 | tf_op jit(solution)/shard_map/convert_element_type | solution.py:47
  61.7 8.1 %all-to-all-done.1 = bf16[128,4,2048]{2,0,1:T(8,128)(2,1)} async-done(((bf16[128,4,2048]{2,0,1:T(8,128)(2,1)}), bf16[128,4,2048]{2,0,1:T(8,128)(2,1)}, u32[]{:S(2)}, u32[]{:S(2)}) %all-to-all-start.1) | async-done | bytes 2097184 | tf_op jit(solution)/shard_map/all_to_all | solution.py:96
  73.3 4.3 %copy.29 = bf16[512,16,128]{0,2,1:T(8,128)(2,1)} copy(bf16[512,16,128]{2,1,0:T(8,128)(2,1)} %bitcast.47) | data formatting | bytes 4194304 | tf_op jit(solution)/shard_map/reshape | solution.py:43
  77.7 11.0 %fusion.9 = f32[16,640,512]{1,2,0:T(8,128)} fusion(bf16[512,16,128]{0,2,1:T(8,128)(2,1)S(1)} %copy.32, bf16[640,16,128]{2,1,0:T(8,128)(2,1)} %bitcast.43), kind=kOutput, calls=%fused_computation.19 | convolution fusion | flops 1342177280 | bytes 25690112 | tf_op jit(solution)/shard_map/thd,khd->htk/dot_general | solution.py:49
  88.7 25.2 %fusion.16 = (f32[16,640]{1,0:T(8,128)S(1)}, f32[16,640,512]{1,2,0:T(8,128)}) fusion(f32[16,640,512]{1,2,0:T(8,128)} %fusion.9, pred[640,512]{0,1:T(8,128)(4,1)S(1)} %broadcast_compare_fusion), kind=kOutput, calls=%fused_computation.29 | output fusion | flops 36700672 | bytes 42311680 | tf_op jit(solution)/shard_map/sub | solution.py:54
  113.9 8.5 %fusion.5 = bf16[16,640,512]{1,2,0:T(8,128)(2,1)S(1)} fusion(f32[16,640,512]{1,2,0:T(8,128)} %get-tuple-element.12, f32[16,640]{1,0:T(8,128)S(1)} %get-tuple-element.11), kind=kLoop, calls=%fused_computation.9 | loop fusion | flops 10485760 | bytes 31498240 | tf_op jit(solution)/shard_map/convert_element_type | solution.py:56
  122.4 6.4 %convert_bitcast_fusion = bf16[512,16,128]{0,2,1:T(8,128)(2,1)} fusion(bf16[640,16,128]{0,2,1:T(8,128)(2,1)} %multiply_convert_fusion.2, bf16[16,640,512]{1,2,0:T(8,128)(2,1)S(1)} %fusion.5), kind=kOutput, calls=%fused_computation.22 | convolution fusion | flops 1343225856 | bytes 15204352 | tf_op jit(solution)/shard_map/htk,thd->khd/dot_general | solution.py:85
  128.9 4.2 %fusion.6 = f32[640,16]{0,1:T(8,128)S(1)} fusion(bf16[640,16,128]{0,2,1:T(8,128)(2,1)} %multiply_convert_fusion.2, bf16[512,16,128]{0,2,1:T(8,128)(2,1)} %copy.29, bf16[16,640,512]{1,2,0:T(8,128)(2,1)S(1)} %fusion.5), kind=kOutput, calls=%fused_computation.12 | convolution fusion | flops 1346099200 | bytes 15245312 | tf_op jit(solution)/shard_map/htk,khd->thd/dot_general | solution.py:57
  133.1 14.2 %multiply_convert_fusion = bf16[16,640,512]{1,2,0:T(8,128)(2,1)} fusion(f32[16,640]{1,0:T(8,128)S(1)} %bitcast.49, f32[16,640,512]{1,2,0:T(8,128)} %get-tuple-element.12, f32[16,640]{1,0:T(8,128)S(1)} %get-tuple-element.11, bf16[512,16,128]{0,2,1:T(8,128)(2,1)} %copy.29, bf16[640,16,128]{0,2,1:T(8,128)(2,1)} %multiply_convert_fusion.2), kind=kOutput, calls=%fused_computation.1 | convolution fusion | flops 1363148800 | bytes 36257792 | tf_op jit(solution)/shard_map/thd,khd->htk/dot_general | solution.py:61
  147.3 7.0 %fusion.11 = bf16[512,16,128]{2,0,1:T(8,128)(2,1)S(1)} fusion(bf16[16,640,512]{1,2,0:T(8,128)(2,1)} %multiply_convert_fusion, bf16[640,16,128]{2,1,0:T(8,128)(2,1)S(1)} %bitcast.44), kind=kOutput, calls=%fused_computation.21 | convolution fusion | flops 1344274432 | bytes 15204352 | tf_op jit(solution)/shard_map/htk,thd->khd/dot_general | solution.py:82
  156.9 4.2 %convert_element_type.57 = bf16[64,8,2048]{2,1,0:T(8,128)(2,1)} reshape(bf16[512,16,128]{2,1,0:T(8,128)(2,1)} %copy.34) | data formatting | bytes 4194304 | tf_op jit(solution)/shard_map/convert_element_type | solution.py:108
  161.1 4.5 %copy.36 = bf16[512,16,128]{2,1,0:T(8,128)(2,1)} copy(bf16[512,16,128]{0,2,1:T(8,128)(2,1)} %convert_bitcast_fusion) | data formatting | bytes 4194304 | tf_op jit(solution)/shard_map/convert_element_type | solution.py:108
  165.6 4.2 %convert_element_type.60 = bf16[64,8,2048]{2,1,0:T(8,128)(2,1)} reshape(bf16[512,16,128]{2,1,0:T(8,128)(2,1)} %copy.36) | data formatting | bytes 4194304 | tf_op jit(solution)/shard_map/convert_element_type | solution.py:108
  169.8 4.7 %pad_maximum_fusion = bf16[64,8,4096]{2,1,0:T(8,128)(2,1)} fusion(bf16[64,8,2048]{2,1,0:T(8,128)(2,1)} %convert_element_type.60, bf16[64,8,2048]{2,1,0:T(8,128)(2,1)} %convert_element_type.57), kind=kLoop, calls=%fused_computation.15 | loop fusion | flops 8388608 | bytes 8388608 | tf_op jit(solution)/shard_map/concatenate | solution.py:21
  174.4 12.3 %all-to-all-start.2 = ((bf16[64,8,4096]{2,1,0:T(8,128)(2,1)}), bf16[64,8,4096]{2,1,0:T(8,128)(2,1)}, u32[]{:S(2)}, u32[]{:S(2)}) async-start(bf16[64,8,4096]{2,1,0:T(8,128)(2,1)} %pad_maximum_fusion), calls=%async_computation.2 | async-start | bytes 8388608 | tf_op jit(solution)/shard_map/all_to_all | solution.py:16
  186.8 7.4 %multiply_convert_fusion.1 = bf16[16,640,128]{1,2,0:T(8,128)(2,1)} fusion(bf16[512,16,128]{0,2,1:T(8,128)(2,1)S(1)} %copy.32, bf16[16,640,512]{1,2,0:T(8,128)(2,1)} %multiply_convert_fusion), kind=kOutput, calls=%fused_computation.13 | convolution fusion | flops 1344798720 | bytes 15204352 | tf_op jit(solution)/shard_map/htk,khd->thd/dot_general | solution.py:68
  194.2 4.4 %copy.37 = bf16[1,640,2048]{2,1,0:T(8,128)(2,1)} copy(bf16[1,640,2048]{1,2,0:T(8,128)(2,1)} %bitcast.42) | data formatting | bytes 5242880
  198.6 83.8 %all-to-all-done.2 = bf16[64,8,4096]{2,1,0:T(8,128)(2,1)} async-done(((bf16[64,8,4096]{2,1,0:T(8,128)(2,1)}), bf16[64,8,4096]{2,1,0:T(8,128)(2,1)}, u32[]{:S(2)}, u32[]{:S(2)}) %all-to-all-start.2) | async-done | bytes 4194336 | tf_op jit(solution)/shard_map/all_to_all | solution.py:16
  (21 shorter events, 25.0 us)
Async XLA Ops:
  6.4 31.6 %all-to-all-start = ((bf16[128,4,2048]{2,0,1:T(8,128)(2,1)}), bf16[128,4,2048]{2,0,1:T(8,128)(2,1)S(1)}, u32[]{:S(2)}, u32[]{:S(2)}) async-start(bf16[128,4,2048]{2,0,1:T(8,128)(2,1)} %copy.21), calls=%async_computation | async-start | bytes 4194304 | tf_op jit(solution)/shard_map/all_to_all | solution.py:95
  19.5 27.3 %copy-start.2 = (s32[1,8]{1,0:T(1,128)S(1)}, s32[1,8]{1,0:T(1,128)}, u32[]{:S(2)}) copy-start(s32[1,8]{1,0:T(1,128)} %param.12) | copy-start | bytes 100
  38.1 31.7 %all-to-all-start.1 = ((bf16[128,4,2048]{2,0,1:T(8,128)(2,1)}), bf16[128,4,2048]{2,0,1:T(8,128)(2,1)}, u32[]{:S(2)}, u32[]{:S(2)}) async-start(bf16[128,4,2048]{2,0,1:T(8,128)(2,1)} %copy.25), calls=%async_computation.1 | async-start | bytes 4194304 | tf_op jit(solution)/shard_map/all_to_all | solution.py:96
  46.8 5.1 %copy-start.3 = (f32[1,16]{1,0:T(1,128)S(1)}, f32[1,16]{1,0:T(1,128)}, u32[]{:S(2)}) copy-start(f32[1,16]{1,0:T(1,128)} %param.11) | copy-start | bytes 196
  46.8 5.1 %copy-start.1 = (s32[640]{0:T(1024)S(1)}, s32[640]{0:T(1024)}, u32[]{:S(2)}) copy-start(s32[640]{0:T(1024)} %param.13) | copy-start | bytes 7684
  133.1 14.2 %copy-start = (bf16[80,8,16,128]{3,2,1,0:T(8,128)(2,1)S(1)}, bf16[80,8,16,128]{3,2,1,0:T(8,128)(2,1)}, u32[]{:S(2)}) copy-start(bf16[80,8,16,128]{3,2,1,0:T(8,128)(2,1)} %copy.44) | copy-start | bytes 7864324
  174.4 107.9 %all-to-all-start.2 = ((bf16[64,8,4096]{2,1,0:T(8,128)(2,1)}), bf16[64,8,4096]{2,1,0:T(8,128)(2,1)}, u32[]{:S(2)}, u32[]{:S(2)}) async-start(bf16[64,8,4096]{2,1,0:T(8,128)(2,1)} %pad_maximum_fusion), calls=%async_computation.2 | async-start | bytes 8388608 | tf_op jit(solution)/shard_map/all_to_all | solution.py:16
where the time goes:
time: 287 us; the launch traced here: 286 us
  waiting for transfers between devices  110 us (38%)
  local copies, waits for them, and re-layouts  57 us (20%)
  matrix products  50.2 us (17%)
  other arithmetic  46 us (16%)
  starting transfers between devices  21.4 us (7%)
    all_to_all x1, waiting for transfers between devices, summed_on_arrival(): lax.all_to_all(blocks, axis, split_axis=0, concat_axis=0, tiled=True)  83.8 us
    sub x1, other arithmetic, attention_grads(): exponent = jnp.where(allowed[None], jnp.exp(masked - row_max), 0.0)  25.2 us
    all_to_all x1, waiting for transfers between devices, shards(): lax.all_to_all(visual_keys[0], 'img', split_axis=1, concat_axis=0, tiled=...  18.6 us
    dot_general x1, matrix products, attention_grads(): jnp.einsum('thd,khd->htk', gated_grad, value_heads, preferred_element_typ...  14.2 us
    unnamed x12, local copies, waits for them, and re-layouts  14 us
    all_to_all x1, starting transfers between devices, summed_on_arrival(): lax.all_to_all(blocks, axis, split_axis=0, concat_axis=0, tiled=True)  12.3 us
    dot_general x1, matrix products, attention_grads(): jnp.einsum('thd,khd->htk', query_heads, key_heads, preferred_element_type...  11 us
    convert_element_type x2, local copies, waits for them, and re-layouts, shards(): value_part.astype(jnp.bfloat16)  8.68 us
  transfers between devices with their start and end apart: 3, of which 3 were waited for; matrix products, arithmetic and copies ran while one was open for 12% of the time, Pallas kernels for 0%

commit v1 on v0

v1 whole, which is shorter than its diff:
```python
import functools
import math

import jax
import jax.numpy as jnp
from jax import lax
from jax.experimental import pallas as pl
from jax.experimental.pallas import tpu as pltpu
from jax.sharding import Mesh, PartitionSpec as P

HEAD = 128
NT = (((1,), (1,)), ((), ()))
NN = (((1,), (0,)), ((), ()))
TN = (((0,), (0,)), ((), ()))
LOG2E = math.log2(math.e)
CHUNKS = 1
AXES = ("yh", "c", "x", "yl", "z")


def head_grads(query, grad_in, keys, values, factor, allowed, scale):
    gated = (grad_in.astype(jnp.float32) * factor).astype(jnp.bfloat16)
    block = keys.shape[0] // len(allowed)
    scores = lax.dot_general(keys, query, NT, preferred_element_type=jnp.float32)
    scores = jnp.concatenate(
        [jnp.where(a, scores[b * block : (b + 1) * block], -1e30) for b, a in enumerate(allowed)], axis=0
    )
    top = jnp.max(scores, axis=0, keepdims=True)
    exponent = jnp.exp2((scores - top) * (scale * LOG2E))
    weights = exponent * (1.0 / jnp.sum(exponent, axis=0, keepdims=True))
    weights_half = weights.astype(jnp.bfloat16)
    weight_grad = lax.dot_general(values, gated, NT, preferred_element_type=jnp.float32)
    row_delta = jnp.sum(weights_half.astype(jnp.float32) * weight_grad, axis=0, keepdims=True)
    score_half = (weights * (weight_grad - row_delta)).astype(jnp.bfloat16)
    query_part = lax.dot_general(keys, score_half, TN, preferred_element_type=jnp.float32) * scale
    key_part = lax.dot_general(score_half, query, NN, preferred_element_type=jnp.float32) * scale
    value_part = lax.dot_general(weights_half, gated, NN, preferred_element_type=jnp.float32)
    return jnp.transpose(query_part), key_part, value_part


def attention_body(
    place, order, factor, seen, query, grad_in, key_own, value_own, key_pair, value_pair,
    unit_0, unit_1, unit_2, unit_3, *rest, first, scale,
):
    query_out, key_send, key_keep, value_send, value_keep, latents, key_rows, value_rows = rest[-8:]
    head = first + pl.program_id(0)
    sources = (key_own, value_own, key_pair, value_pair, unit_0, unit_1, unit_2, unit_3)
    for i, source in enumerate(sources):
        latents[pl.ds(pl.multiple_of(place[1 + i], 128), 128), :] = source[...].reshape(128, HEAD)
    allowed = [order[b] < seen[...] for b in range(8)]
    total = latents.shape[0] // 2
    query_part, key_part, value_part = head_grads(
        query[...], grad_in[...], latents[:total], latents[total:], factor[head], allowed, scale
    )
    query_out[...] = query_part.astype(jnp.bfloat16)
    key_rows[...] = key_part.astype(jnp.bfloat16)
    value_rows[...] = value_part.astype(jnp.bfloat16)
    for rows, outs, at in ((key_rows, (key_send, key_keep), 9), (value_rows, (value_send, value_keep), 13)):
        for i in range(4):
            outs[i // 2][pl.ds(i % 2 * 128, 128), :] = rows[pl.ds(pl.multiple_of(place[at + i], 128), 128), :]


def attention(place, order, factor, seen, query, grad_in, key_own, value_own, pair, units, buffer, first, count):
    tokens = query.shape[0]
    scalar = pl.BlockSpec(memory_space=pltpu.SMEM)
    head_of = lambda h, place: (0, first + h)
    own_of = lambda h, place: (0, place[0] + first + h)
    part = lambda rows: pl.BlockSpec((rows, HEAD), lambda h, place: (0, h))
    grads = jax.ShapeDtypeStruct((256, count * HEAD), jnp.bfloat16)
    grid_spec = pltpu.PrefetchScalarGridSpec(
        num_scalar_prefetch=1,
        grid=(count,),
        in_specs=[
            scalar,
            scalar,
            pl.BlockSpec((1, tokens), lambda h, place: (0, 0)),
            pl.BlockSpec((tokens, HEAD), head_of),
            pl.BlockSpec((tokens, HEAD), head_of),
            pl.BlockSpec((128, HEAD), own_of),
            pl.BlockSpec((128, HEAD), own_of),
            pl.BlockSpec((1, 128, HEAD), lambda h, place: (0, 0, h)),
            pl.BlockSpec((1, 128, HEAD), lambda h, place: (1, 0, h)),
            part(128),
            part(128),
            part(128),
            part(128),
        ] + [pl.BlockSpec(memory_space=pl.ANY)] * len(buffer),
        out_specs=[pl.BlockSpec((tokens, HEAD), head_of)] + [part(256)] * 4,
        scratch_shapes=[
            pltpu.VMEM((1024, HEAD), jnp.bfloat16),
            pltpu.VMEM((512, HEAD), jnp.bfloat16),
            pltpu.VMEM((512, HEAD), jnp.bfloat16),
        ],
    )
    matmul = 2 * tokens * 512 * HEAD
    return pl.pallas_call(
        functools.partial(attention_body, first=first, scale=1.0 / math.sqrt(HEAD)),
        grid_spec=grid_spec,
        out_shape=[jax.ShapeDtypeStruct(query.shape, jnp.bfloat16)] + [grads] * 4,
        input_output_aliases={14: 0} if buffer else {},
        compiler_params=pltpu.CompilerParams(
            dimension_semantics=("arbitrary",), vmem_limit_bytes=48 * 2**20
        ),
        cost_estimate=pl.CostEstimate(
            flops=5 * count * matmul, transcendentals=count * tokens * 512, bytes_accessed=count * 2**20
        ),
        name="attention",
    )(place, order, factor, seen, query, grad_in, key_own, value_own, pair, pair, *units, *buffer)


def relabel(sizes, move):
    pairs = []
    total = math.prod(sizes)
    for source in range(total):
        rest, at = source, []
        for size in reversed(sizes):
            at.append(rest % size)
            rest //= size
        to = 0
        for index, size in zip(move(*reversed(at)), sizes):
            to = to * size + index % size
        pairs.append((source, to))
    return pairs


def columns(array, start, width):
    return lax.dynamic_slice(array, (0, start), (array.shape[0], width))


def shards(queries, visual_keys, visual_values, out_grad, gate_value, image_order, image_seen):
    query, grad_in, keys, values = queries[0], out_grad[0], visual_keys[0], visual_values[0]
    local = query.shape[1]
    heads = local // HEAD
    yh, c, x, yl, z = (lax.axis_index(a) for a in AXES)
    colour = lambda x, z, c: (x + 2 * z) % 4 ^ c
    row_block = lambda owner: owner * 128
    unit_at = lambda unit: unit // 2 * 512 + row_block((1 - yh) * 2 + unit % 2)
    own = yh * 2 + c
    pair_owner = yh * 2 + 1 - c
    place = [own * heads, row_block(own), 512 + row_block(own), row_block(pair_owner), 512 + row_block(pair_owner)]
    place += [unit_at(colour(x + dx, z + dz, c)) for dx, dz in ((0, 0), (3, 0), (1, 0), (0, 7))]
    step = x ^ 1
    cross = 3 - x
    place += [row_block(b) for b in (3 - step, step, cross, x)]
    place += [row_block(b) for b in (cross ^ 1, cross, step, x)]
    place = jnp.stack(place).astype(jnp.int32)
    factor = jnp.tanh(gate_value[0])
    seen = image_seen[None]

    to_cross = relabel((2, 2, 4, 2), lambda yh, c, x, yl: (1 - yh, c ^ (x & 1), x, 1 - yl))
    flip_pairs = [(i, i ^ 1) for i in range(4)]
    cross_pairs = [(i, 3 - i) for i in range(4)]
    there = (1 - yh) * 2 + (c ^ (x & 1))
    wants_values = (x + 2 * z) % 4 // 2 == 1

    count = heads // CHUNKS
    width = count * HEAD
    gathered = []
    for n in range(CHUNKS):
        at = n * width
        pair = jnp.stack([columns(a, pair_owner * local + at, width) for a in (keys, values)])
        pair = lax.ppermute(pair, "c", [(0, 1), (1, 0)])
        sent = jnp.where(
            wants_values, columns(values, there * local + at, width), columns(keys, there * local + at, width)
        )
        unit = lax.ppermute(sent, ("yh", "c", "x", "yl"), to_cross)
        units = [
            unit,
            lax.ppermute(unit, "x", [(i, (i + 1) % 4) for i in range(4)]),
            lax.ppermute(unit, "x", [(i, (i + 3) % 4) for i in range(4)]),
            lax.ppermute(unit, "z", [(i, (i + 1) % 8) for i in range(8)]),
        ]
        gathered.append((pair, units))

    query_grad = ()
    parts = []
    f32 = jnp.float32
    for n in range(CHUNKS):
        pair, units = gathered[n]
        whole, key_send, key_keep, value_send, value_keep = attention(
            place, image_order[0], factor, seen, query, grad_in, keys, values, pair, units,
            query_grad, n * count, count,
        )
        query_grad = (whole,)
        mine = []
        for send, keep, first, second in (
            (key_send, key_keep, flip_pairs, cross_pairs),
            (value_send, value_keep, cross_pairs, flip_pairs),
        ):
            got = lax.ppermute(send, "x", first)
            passed = (keep[:128].astype(f32) + got[:128].astype(f32)).astype(jnp.bfloat16)
            passed = lax.ppermute(passed, "x", second)
            mine.append(
                (keep[128:].astype(f32) + got[128:].astype(f32) + passed.astype(f32)).astype(jnp.bfloat16)
            )
        both = jnp.stack([m.reshape(16, 8, width) for m in mine], axis=1)
        arrived = lax.all_to_all(both, ("yl", "z"), split_axis=0, concat_axis=0, tiled=True)
        parts.append(arrived.astype(f32).sum(axis=0))
    result = jnp.concatenate(parts, axis=2)
    return whole[None], result[0][None], result[1][None]


def solution(mesh):
    torus = Mesh(mesh.devices.reshape(2, 2, 4, 2, 8), AXES)
    img, txt = ("yh", "c"), ("x", "yl", "z")
    placed = (
        P(None, txt, img),
        P(None, img, None),
        P(None, img, None),
        P(None, txt, img),
        P(None, img),
        P(),
        P(txt),
    )
    return jax.shard_map(
        shards, mesh=torus, in_specs=placed, out_specs=(P(None, txt, img),) * 3, check_vma=False
    )
```

time: 287 us -> 139 us (0.48)
  local copies, waits for them, and re-layouts: 57 us -> 0.78 us
  waiting for transfers between devices: 110 us -> 58.1 us
  matrix products: 50.2 us -> 0 us
  other arithmetic: 46 us -> 3.94 us
  Pallas kernels: 0 us -> 29.6 us
  blocking collectives: 0 us -> 29.2 us
  starting transfers between devices: 21.4 us -> 13.5 us
    all_to_all x3 -> x0, waiting for transfers between devices: 110 us -> none  [the longest x1 83.8 us: summed_on_arrival(): lax.all_to_all(blocks, axis, split_axis=0, concat_axis=0, tiled=True)]
    ppermute x0 -> x9, waiting for transfers between devices: none -> 58.1 us  [the longest x2 21.9 us: shards(): got = lax.ppermute(send, 'x', first)]
    dot_general x6 -> x0, matrix products: 50.2 us -> none  [the longest x1 14.2 us: attention_grads(): jnp.einsum('thd,khd->htk', gated_grad, value_heads, preferred_element_typ...]
    pallas_call x0 -> x1, Pallas kernels: none -> 29.6 us  [attention(): pl.pallas_call(functools.partial(attention_body, first=first, scale=1.0 /...]
    all_to_all x0 -> x1, blocking collectives: none -> 29.2 us  [shards(): lax.all_to_all(both, ('yl', 'z'), split_axis=0, concat_axis=0, tiled=True)]
    sub x1 -> x0, other arithmetic: 25.2 us -> none  [attention_grads(): exponent = jnp.where(allowed[None], jnp.exp(masked - row_max), 0.0)]
    all_to_all x3 -> x0, starting transfers between devices: 21.4 us -> none  [the longest x1 12.3 us: summed_on_arrival(): lax.all_to_all(blocks, axis, split_axis=0, concat_axis=0, tiled=True)]
    convert_element_type x5 -> x0, local copies, waits for them, and re-layouts: 20.4 us -> none  [the longest x2 8.68 us: shards(): value_part.astype(jnp.bfloat16)]
  transfers between devices with their start and end apart: 3 -> 9, of which waited for: 3 -> 5; matrix products, arithmetic and copies ran while one was open for 12% -> 1% of each run, Pallas kernels for 0% -> 0%
where the time goes in v1:
time: 139 us; the launch traced here: 136 us
  waiting for transfers between devices  58.1 us (42%)
  Pallas kernels  29.6 us (21%)
  blocking collectives  29.2 us (21%)
  starting transfers between devices  13.5 us (10%)
  other arithmetic  3.94 us (3%)
    pallas_call x1, Pallas kernels, attention(): pl.pallas_call(functools.partial(attention_body, first=first, scale=1.0 /...  29.6 us
    all_to_all x1, blocking collectives, shards(): lax.all_to_all(both, ('yl', 'z'), split_axis=0, concat_axis=0, tiled=True)  29.2 us
    ppermute x2, waiting for transfers between devices, shards(): got = lax.ppermute(send, 'x', first)  21.9 us
    ppermute x1, waiting for transfers between devices, shards(): lax.ppermute(unit, 'z', [(i, (i + 1) % 8) for i in range(8)])  14.1 us
    ppermute x1, waiting for transfers between devices, shards(): unit = lax.ppermute(sent, ('yh', 'c', 'x', 'yl'), to_cross)  11.8 us
    ppermute x2, waiting for transfers between devices, shards(): passed = lax.ppermute(passed, 'x', second)  10.3 us
    ppermute x2, starting transfers between devices, shards(): passed = lax.ppermute(passed, 'x', second)  3.53 us
  transfers between devices with their start and end apart: 9, of which 5 were waited for; matrix products, arithmetic and copies ran while one was open for 1% of the time, Pallas kernels for 0%

profile of v1, /device:TPU:2, one launch (start us, length us, event | category | flops | bytes accessed | tf_op | source)
XLA Modules:
  0.0 135.9 jit_solution(11080832676357884872)
XLA Ops:
  0.7 1.8 %select_bitcast_fusion = (bf16[128,2048]{1,0:T(8,128)(2,1)S(1)}, bf16[1,128,2048]{2,1,0:T(8,128)(2,1)S(1)}, bf16[1,128,2048]{2,1,0:T(8,128)(2,1)S(1)}) fusion(bf16[1,128,8192]{2,1,0:T(8,128)(2,1)} %param.8, s32[]{:T(128)S(6)} %select_n.87, bf16[1,128,8192]{2,1,0:T(8,128)(2,1)} %param.9, pred[]{:T(512)S(6)} %eq.13, s32[]{:T(128)S(6)} %select_n.84), kind=kLoop, calls=%fused_computation.9 | loop fusion | flops 262144 | bytes 3670025 | tf_op jit(solution)/shard_map/jit(_where)/select_n | solution.py:162
  2.5 2.5 %collective-permute-start.1 = (bf16[128,2048]{1,0:T(8,128)(2,1)S(1)}, bf16[128,2048]{1,0:T(8,128)(2,1)S(1)}, u32[]{:S(2)}, u32[]{:S(2)}) collective-permute-start(bf16[128,2048]{1,0:T(8,128)(2,1)S(1)} %get-tuple-element.13), channel_id=1, source_target_pairs={{0,136},{8,128},{16,216},{24,208},{32,168},{40,160},{48,248},{56,2... | collective-permute-start | bytes 1572872 | tf_op jit(solution)/shard_map/ppermute | solution.py:165
  5.2 0.8 collective-permute-start
  5.9 11.8 %collective-permute-done.1.unit_0 = bf16[128,2048]{1,0:T(8,128)(2,1)S(1)} collective-permute-done((bf16[128,2048]{1,0:T(8,128)(2,1)S(1)}, bf16[128,2048]{1,0:T(8,128)(2,1)S(1)}, u32[]{:S(2)}, u32[]{:S(2)}) %collective-permute-start.1) | collective-permute-done | bytes 524320 | tf_op jit(solution)/shard_map/ppermute | solution.py:165
  17.7 1.9 %collective-permute-start.4 = (bf16[128,2048]{1,0:T(8,128)(2,1)S(1)}, bf16[128,2048]{1,0:T(8,128)(2,1)S(1)}, u32[]{:S(2)}, u32[]{:S(2)}) collective-permute-start(bf16[128,2048]{1,0:T(8,128)(2,1)S(1)} %collective-permute-done.1.unit_0), channel_id=1, source_target_pairs={{0,1},{1,2},{2,3},{3,4},{4,5},{5,6},{6,7},{7,0},{8,9},{9,10},{10,1... | collective-permute-start | bytes 1572872 | tf_op jit(solution)/shard_map/ppermute | solution.py:170
  19.6 0.4 collective-permute-start.3
  20.0 1.6 %collective-permute-start.2 = (bf16[128,2048]{1,0:T(8,128)(2,1)S(1)}, bf16[128,2048]{1,0:T(8,128)(2,1)S(1)}, u32[]{:S(2)}, u32[]{:S(2)}) collective-permute-start(bf16[128,2048]{1,0:T(8,128)(2,1)S(1)} %collective-permute-done.1.unit_0), channel_id=1, source_target_pairs={{0,16},{16,32},{32,48},{48,0},{1,17},{17,33},{33,49},{49,1},{2,18}... | collective-permute-start | bytes 1572872 | tf_op jit(solution)/shard_map/ppermute | solution.py:168
  21.8 14.1 %collective-permute-done.4.unit_3 = bf16[128,2048]{1,0:T(8,128)(2,1)S(1)} collective-permute-done((bf16[128,2048]{1,0:T(8,128)(2,1)S(1)}, bf16[128,2048]{1,0:T(8,128)(2,1)S(1)}, u32[]{:S(2)}, u32[]{:S(2)}) %collective-permute-start.4) | collective-permute-done | bytes 524320 | tf_op jit(solution)/shard_map/ppermute | solution.py:170
  35.8 29.6 %attention.1 = (bf16[640,2048]{1,0:T(8,128)(2,1)}, bf16[256,2048]{1,0:T(8,128)(2,1)S(1)}, bf16[256,2048]{1,0:T(8,128)(2,1)S(1)}, bf16[256,2048]{1,0:T(8,128)(2,1)S(1)}, bf16[256,2048]{1,0:T(8,128)(2,1)}) custom-call(s32[17]{0:T(128)S(1)} %stack.70.place, s32[8]{0:T(128)S(1)} %bitcast.32, f32[16]{0:T(128)S(1)} %tanh_bitcast_fusion.factor, ...), custom_call_target="tpu_custom_call" | custom-call | flops 6710886400 | bytes 16777216 | tf_op jit(solution)/shard_map/attention/pallas_call | solution.py:95
  65.4 1.8 %collective-permute-start.5 = (bf16[256,2048]{1,0:T(8,128)(2,1)S(1)}, bf16[256,2048]{1,0:T(8,128)(2,1)S(1)}, u32[]{:S(2)}, u32[]{:S(2)}) collective-permute-start(bf16[256,2048]{1,0:T(8,128)(2,1)S(1)} %get-tuple-element.10), channel_id=1, source_target_pairs={{0,16},{16,0},{32,48},{48,32},{1,17},{17,1},{33,49},{49,33},{2,18}... | collective-permute-start | bytes 3145736 | tf_op jit(solution)/shard_map/ppermute | solution.py:189
  67.2 1.0 collective-permute-start.7
  68.2 21.9 %collective-permute-done.5 = bf16[256,2048]{1,0:T(8,128)(2,1)S(1)} collective-permute-done((bf16[256,2048]{1,0:T(8,128)(2,1)S(1)}, bf16[256,2048]{1,0:T(8,128)(2,1)S(1)}, u32[]{:S(2)}, u32[]{:S(2)}) %collective-permute-start.5) | collective-permute-done | bytes 1048608 | tf_op jit(solution)/shard_map/ppermute | solution.py:189
  90.1 0.1 add_convert_fusion.3
  90.2 1.1 collective-permute-start.6
  91.3 1.2 add_convert_fusion.1
  92.5 2.4 %collective-permute-start.8 = (bf16[128,2048]{1,0:T(8,128)(2,1)S(1)}, bf16[128,2048]{1,0:T(8,128)(2,1)S(1)}, u32[]{:S(2)}, u32[]{:S(2)}) collective-permute-start(bf16[128,2048]{1,0:T(8,128)(2,1)S(1)} %add_convert_fusion.1), channel_id=1, source_target_pairs={{0,16},{16,0},{32,48},{48,32},{1,17},{17,1},{33,49},{49,33},{2,18}... | collective-permute-start | bytes 1572872 | tf_op jit(solution)/shard_map/ppermute | solution.py:191
  94.9 7.9 %collective-permute-done.6 = bf16[128,2048]{1,0:T(8,128)(2,1)S(1)} collective-permute-done((bf16[128,2048]{1,0:T(8,128)(2,1)S(1)}, bf16[128,2048]{1,0:T(8,128)(2,1)S(1)}, u32[]{:S(2)}, u32[]{:S(2)}) %collective-permute-start.6) | collective-permute-done | bytes 524320 | tf_op jit(solution)/shard_map/ppermute | solution.py:191
  102.8 0.2 fusion
  103.1 2.4 %collective-permute-done.8 = bf16[128,2048]{1,0:T(8,128)(2,1)S(1)} collective-permute-done((bf16[128,2048]{1,0:T(8,128)(2,1)S(1)}, bf16[128,2048]{1,0:T(8,128)(2,1)S(1)}, u32[]{:S(2)}, u32[]{:S(2)}) %collective-permute-start.8) | collective-permute-done | bytes 524320 | tf_op jit(solution)/shard_map/ppermute | solution.py:191
  105.5 0.2 fusion.1
  105.8 0.1 pad_maximum_fusion.1
  105.9 29.2 %all_to_all.5 = bf16[16,2,8,2048]{3,2,1,0:T(8,128)(2,1)S(1)} all-to-all(bf16[16,2,8,2048]{3,2,1,0:T(8,128)(2,1)S(1)} %pad_maximum_fusion.1), channel_id=1, replica_groups=mesh['yh'=2,'c'=2,'x'=4,'yl'=2,'z'=8] {'yl','z'}, dimensions={0} | all-to-all | bytes 2097152 | tf_op jit(solution)/shard_map/all_to_all | solution.py:196
  135.0 0.1 convert_reduce_fusion
  135.2 0.7 fusion.2
  (16 shorter events, 0.2 us)
Async XLA Ops:
  2.5 19.1 %copy-start.2 = (s32[640]{0:T(1024)S(1)}, s32[640]{0:T(1024)}, u32[]{:S(2)}) copy-start(s32[640]{0:T(1024)} %param.13) | copy-start | bytes 7684
  2.5 19.2 %copy-start.3 = (f32[1,16]{1,0:T(1,128)S(1)}, f32[1,16]{1,0:T(1,128)}, u32[]{:S(2)}) copy-start(f32[1,16]{1,0:T(1,128)} %param.11) | copy-start | bytes 196
  2.5 33.3 %copy-start = (s32[1,8]{1,0:T(1,128)S(1)}, s32[1,8]{1,0:T(1,128)}, u32[]{:S(2)}) copy-start(s32[1,8]{1,0:T(1,128)} %param.12) | copy-start | bytes 100
  2.5 15.2 %collective-permute-start.1 = (bf16[128,2048]{1,0:T(8,128)(2,1)S(1)}, bf16[128,2048]{1,0:T(8,128)(2,1)S(1)}, u32[]{:S(2)}, u32[]{:S(2)}) collective-permute-start(bf16[128,2048]{1,0:T(8,128)(2,1)S(1)} %get-tuple-element.13), channel_id=1, source_target_pairs={{0,136},{8,128},{16,216},{24,208},{32,168},{40,160},{48,248},{56,2... | collective-permute-start | bytes 1572872 | tf_op jit(solution)/shard_map/ppermute | solution.py:165
  5.2 30.7 %collective-permute-start = (bf16[2,128,2048]{2,1,0:T(8,128)(2,1)S(1)}, bf16[2,128,2048]{2,1,0:T(8,128)(2,1)}, u32[]{:S(2)}, u32[]{:S(2)}) collective-permute-start(bf16[2,128,2048]{2,1,0:T(8,128)(2,1)S(1)} %pad_maximum_fusion), channel_id=1, source_target_pairs={{0,64},{64,0},{1,65},{65,1},{2,66},{66,2},{3,67},{67,3},{4,68},{68... | collective-permute-start | bytes 3145736 | tf_op jit(solution)/shard_map/ppermute | solution.py:161
  17.7 18.1 %collective-permute-start.4 = (bf16[128,2048]{1,0:T(8,128)(2,1)S(1)}, bf16[128,2048]{1,0:T(8,128)(2,1)S(1)}, u32[]{:S(2)}, u32[]{:S(2)}) collective-permute-start(bf16[128,2048]{1,0:T(8,128)(2,1)S(1)} %collective-permute-done.1.unit_0), channel_id=1, source_target_pairs={{0,1},{1,2},{2,3},{3,4},{4,5},{5,6},{6,7},{7,0},{8,9},{9,10},{10,1... | collective-permute-start | bytes 1572872 | tf_op jit(solution)/shard_map/ppermute | solution.py:170
  19.6 16.2 %collective-permute-start.3 = (bf16[128,2048]{1,0:T(8,128)(2,1)S(1)}, bf16[128,2048]{1,0:T(8,128)(2,1)S(1)}, u32[]{:S(2)}, u32[]{:S(2)}) collective-permute-start(bf16[128,2048]{1,0:T(8,128)(2,1)S(1)} %collective-permute-done.1.unit_0), channel_id=1, source_target_pairs={{0,48},{16,0},{32,16},{48,32},{1,49},{17,1},{33,17},{49,33},{2,50}... | collective-permute-start | bytes 1572872 | tf_op jit(solution)/shard_map/ppermute | solution.py:169
  20.0 15.8 %collective-permute-start.2 = (bf16[128,2048]{1,0:T(8,128)(2,1)S(1)}, bf16[128,2048]{1,0:T(8,128)(2,1)S(1)}, u32[]{:S(2)}, u32[]{:S(2)}) collective-permute-start(bf16[128,2048]{1,0:T(8,128)(2,1)S(1)} %collective-permute-done.1.unit_0), channel_id=1, source_target_pairs={{0,16},{16,32},{32,48},{48,0},{1,17},{17,33},{33,49},{49,1},{2,18}... | collective-permute-start | bytes 1572872 | tf_op jit(solution)/shard_map/ppermute | solution.py:168
  65.4 24.7 %collective-permute-start.5 = (bf16[256,2048]{1,0:T(8,128)(2,1)S(1)}, bf16[256,2048]{1,0:T(8,128)(2,1)S(1)}, u32[]{:S(2)}, u32[]{:S(2)}) collective-permute-start(bf16[256,2048]{1,0:T(8,128)(2,1)S(1)} %get-tuple-element.10), channel_id=1, source_target_pairs={{0,16},{16,0},{32,48},{48,32},{1,17},{17,1},{33,49},{49,33},{2,18}... | collective-permute-start | bytes 3145736 | tf_op jit(solution)/shard_map/ppermute | solution.py:189
  67.2 24.1 %collective-permute-start.7 = (bf16[256,2048]{1,0:T(8,128)(2,1)S(1)}, bf16[256,2048]{1,0:T(8,128)(2,1)S(1)}, u32[]{:S(2)}, u32[]{:S(2)}) collective-permute-start(bf16[256,2048]{1,0:T(8,128)(2,1)S(1)} %get-tuple-element.12), channel_id=1, source_target_pairs={{0,48},{16,32},{32,16},{48,0},{1,49},{17,33},{33,17},{49,1},{2,50}... | collective-permute-start | bytes 3145736 | tf_op jit(solution)/shard_map/ppermute | solution.py:189
  90.2 15.3 %copy-start.1 = (bf16[256,2048]{1,0:T(8,128)(2,1)S(1)}, bf16[256,2048]{1,0:T(8,128)(2,1)}, u32[]{:S(2)}) copy-start(bf16[256,2048]{1,0:T(8,128)(2,1)} %get-tuple-element.11) | copy-start | bytes 3145732
  90.2 12.6 %collective-permute-start.6 = (bf16[128,2048]{1,0:T(8,128)(2,1)S(1)}, bf16[128,2048]{1,0:T(8,128)(2,1)S(1)}, u32[]{:S(2)}, u32[]{:S(2)}) collective-permute-start(bf16[128,2048]{1,0:T(8,128)(2,1)S(1)} %add_convert_fusion.3), channel_id=1, source_target_pairs={{0,48},{16,32},{32,16},{48,0},{1,49},{17,33},{33,17},{49,1},{2,50}... | collective-permute-start | bytes 1572872 | tf_op jit(solution)/shard_map/ppermute | solution.py:191
  92.5 13.0 %collective-permute-start.8 = (bf16[128,2048]{1,0:T(8,128)(2,1)S(1)}, bf16[128,2048]{1,0:T(8,128)(2,1)S(1)}, u32[]{:S(2)}, u32[]{:S(2)}) collective-permute-start(bf16[128,2048]{1,0:T(8,128)(2,1)S(1)} %add_convert_fusion.1), channel_id=1, source_target_pairs={{0,16},{16,0},{32,48},{48,32},{1,17},{17,1},{33,49},{49,33},{2,18}... | collective-permute-start | bytes 1572872 | tf_op jit(solution)/shard_map/ppermute | solution.py:191

commit v2 on v1

--- a/solution.py
+++ b/solution.py
@@ -8,12 +8,14 @@
 from jax.experimental.pallas import tpu as pltpu
 from jax.sharding import Mesh, PartitionSpec as P
 
+
 HEAD = 128
 NT = (((1,), (1,)), ((), ()))
 NN = (((1,), (0,)), ((), ()))
 TN = (((0,), (0,)), ((), ()))
 LOG2E = math.log2(math.e)
-CHUNKS = 1
+GATHERS = ((6,), (4, 3, 3))
+PLANES = ((0,), (1, 2, 3))
 AXES = ("yh", "c", "x", "yl", "z")
 
 
@@ -59,12 +61,12 @@
             outs[i // 2][pl.ds(i % 2 * 128, 128), :] = rows[pl.ds(pl.multiple_of(place[at + i], 128), 128), :]
 
 
-def attention(place, order, factor, seen, query, grad_in, key_own, value_own, pair, units, buffer, first, count):
+def attention(place, order, factor, seen, query, grad_in, key_own, value_own, pair, units, buffer, first, count, offset):
     tokens = query.shape[0]
     scalar = pl.BlockSpec(memory_space=pltpu.SMEM)
     head_of = lambda h, place: (0, first + h)
     own_of = lambda h, place: (0, place[0] + first + h)
-    part = lambda rows: pl.BlockSpec((rows, HEAD), lambda h, place: (0, h))
+    part = lambda rows, at=0: pl.BlockSpec((rows, HEAD), lambda h, place: (0, at + h))
     grads = jax.ShapeDtypeStruct((256, count * HEAD), jnp.bfloat16)
     grid_spec = pltpu.PrefetchScalarGridSpec(
         num_scalar_prefetch=1,
@@ -77,12 +79,12 @@
             pl.BlockSpec((tokens, HEAD), head_of),
             pl.BlockSpec((128, HEAD), own_of),
             pl.BlockSpec((128, HEAD), own_of),
-            pl.BlockSpec((1, 128, HEAD), lambda h, place: (0, 0, h)),
-            pl.BlockSpec((1, 128, HEAD), lambda h, place: (1, 0, h)),
-            part(128),
-            part(128),
-            part(128),
-            part(128),
+            pl.BlockSpec((1, 128, HEAD), lambda h, place: (0, 0, offset + h)),
+            pl.BlockSpec((1, 128, HEAD), lambda h, place: (1, 0, offset + h)),
+            part(128, offset),
+            part(128, offset),
+            part(128, offset),
+            part(128, offset),
         ] + [pl.BlockSpec(memory_space=pl.ANY)] * len(buffer),
         out_specs=[pl.BlockSpec((tokens, HEAD), head_of)] + [part(256)] * 4,
         scratch_shapes=[
@@ -130,7 +132,7 @@
     query, grad_in, keys, values = queries[0], out_grad[0], visual_keys[0], visual_values[0]
     local = query.shape[1]
     heads = local // HEAD
-    yh, c, x, yl, z = (lax.axis_index(a) for a in AXES)
+    yh, c, x, _, z = (lax.axis_index(a) for a in AXES)
     colour = lambda x, z, c: (x + 2 * z) % 4 ^ c
     row_block = lambda owner: owner * 128
     unit_at = lambda unit: unit // 2 * 512 + row_block((1 - yh) * 2 + unit % 2)
@@ -152,47 +154,47 @@
     there = (1 - yh) * 2 + (c ^ (x & 1))
     wants_values = (x + 2 * z) % 4 // 2 == 1
 
-    count = heads // CHUNKS
-    width = count * HEAD
     gathered = []
-    for n in range(CHUNKS):
-        at = n * width
-        pair = jnp.stack([columns(a, pair_owner * local + at, width) for a in (keys, values)])
-        pair = lax.ppermute(pair, "c", [(0, 1), (1, 0)])
+    first = 0
+    for counts in GATHERS:
+        at, width = first * HEAD, sum(counts) * HEAD
         sent = jnp.where(
             wants_values, columns(values, there * local + at, width), columns(keys, there * local + at, width)
         )
+        pair = jnp.stack([columns(a, pair_owner * local + at, width) for a in (keys, values)])
         unit = lax.ppermute(sent, ("yh", "c", "x", "yl"), to_cross)
-        units = [
-            unit,
-            lax.ppermute(unit, "x", [(i, (i + 1) % 4) for i in range(4)]),
-            lax.ppermute(unit, "x", [(i, (i + 3) % 4) for i in range(4)]),
-            lax.ppermute(unit, "z", [(i, (i + 1) % 8) for i in range(8)]),
-        ]
-        gathered.append((pair, units))
-
-    query_grad = ()
-    parts = []
+        pair = lax.ppermute(pair, "c", [(0, 1), (1, 0)])
+        units = [unit]
+        for axis, size, by in (("x", 4, 1), ("x", 4, 3), ("z", 8, 1)):
+            units.append(lax.ppermute(unit, axis, [(i, (i + by) % size) for i in range(size)]))
+        offset = 0
+        for count in counts:
+            gathered.append((pair, units, first, count, offset))
+            first += count
+            offset += count
+
+    buffer = ()
+    ready, parts = [], []
     f32 = jnp.float32
-    for n in range(CHUNKS):
-        pair, units = gathered[n]
+    for pair, units, first, count, offset in gathered:
         whole, key_send, key_keep, value_send, value_keep = attention(
             place, image_order[0], factor, seen, query, grad_in, keys, values, pair, units,
-            query_grad, n * count, count,
+            buffer, first, count, offset,
         )
-        query_grad = (whole,)
+        buffer = (whole,)
         mine = []
-        for send, keep, first, second in (
-            (key_send, key_keep, flip_pairs, cross_pairs),
-            (value_send, value_keep, cross_pairs, flip_pairs),
+        for send, keep, near, far in (
+            (key_send, key_keep, flip_pairs, cross_pairs), (value_send, value_keep, cross_pairs, flip_pairs)
         ):
-            got = lax.ppermute(send, "x", first)
+            got = lax.ppermute(send, "x", near)
             passed = (keep[:128].astype(f32) + got[:128].astype(f32)).astype(jnp.bfloat16)
-            passed = lax.ppermute(passed, "x", second)
+            passed = lax.ppermute(passed, "x", far)
             mine.append(
                 (keep[128:].astype(f32) + got[128:].astype(f32) + passed.astype(f32)).astype(jnp.bfloat16)
             )
-        both = jnp.stack([m.reshape(16, 8, width) for m in mine], axis=1)
+        ready.append(jnp.stack([m.reshape(16, 8, count * HEAD) for m in mine], axis=1))
+    for members in PLANES:
+        both = jnp.concatenate([ready[m] for m in members], axis=3)
         arrived = lax.all_to_all(both, ("yl", "z"), split_axis=0, concat_axis=0, tiled=True)
         parts.append(arrived.astype(f32).sum(axis=0))
     result = jnp.concatenate(parts, axis=2)
@@ -211,6 +213,4 @@
         P(),
         P(txt),
     )
-    return jax.shard_map(
-        shards, mesh=torus, in_specs=placed, out_specs=(P(None, txt, img),) * 3, check_vma=False
-    )
+    return jax.shard_map(shards, mesh=torus, in_specs=placed, out_specs=(P(None, txt, img),) * 3, check_vma=False)

time: 139 us -> 135 us (0.971)
  starting transfers between devices: 13.5 us -> 46.6 us
  blocking collectives: 29.2 us -> 0 us
  waiting for transfers between devices: 58.1 us -> 34.8 us
  other arithmetic: 3.94 us -> 9.95 us
  Pallas kernels: 29.6 us -> 35.3 us
  local copies, waits for them, and re-layouts: 0.78 us -> 5.11 us
    ppermute x7 -> x22, waiting for transfers between devices: 46.3 us -> 7.52 us  [the longest x6 3.81 us: shards(): lax.ppermute(unit, axis, [(i, (i + by) % size) for i in range(size)])]
    all_to_all x1 -> x0, blocking collectives: 29.2 us -> none  [shards(): lax.all_to_all(both, ('yl', 'z'), split_axis=0, concat_axis=0, tiled=True)]
    ppermute x7 -> x22, starting transfers between devices: 10.2 us -> 33.9 us  [the longest x8 15.4 us: shards(): passed = lax.ppermute(passed, 'x', far)]
    all_to_all x0 -> x2, waiting for transfers between devices: none -> 19.7 us  [shards(): lax.all_to_all(both, ('yl', 'z'), split_axis=0, concat_axis=0, tiled=True)]
    all_to_all x0 -> x2, starting transfers between devices: none -> 9.49 us  [shards(): lax.all_to_all(both, ('yl', 'z'), split_axis=0, concat_axis=0, tiled=True)]
    pallas_call x1 -> x4, Pallas kernels: 29.6 us -> 35.3 us  [attention(): pl.pallas_call(functools.partial(attention_body, first=first, scale=1.0 /...]
    unnamed x8 -> x36, local copies, waits for them, and re-layouts: 0.02 us -> 5.01 us
    ppermute x1 -> x2, waiting for transfers between devices: 11.8 us -> 7.48 us  [shards(): unit = lax.ppermute(sent, ('yh', 'c', 'x', 'yl'), to_cross)]
  transfers between devices with their start and end apart: 9 -> 28, of which waited for: 5 -> 7; matrix products, arithmetic and copies ran while one was open for 1% -> 5% of each run, Pallas kernels for 0% -> 27%
where the time goes in v2:
time: 135 us; the launch traced here: 133 us
  starting transfers between devices  46.6 us (35%)
  Pallas kernels  35.3 us (26%)
  waiting for transfers between devices  34.8 us (26%)
  other arithmetic  9.95 us (7%)
  local copies, waits for them, and re-layouts  5.11 us (4%)
    pallas_call x4, Pallas kernels, attention(): pl.pallas_call(functools.partial(attention_body, first=first, scale=1.0 /...  35.3 us
    all_to_all x2, waiting for transfers between devices, shards(): lax.all_to_all(both, ('yl', 'z'), split_axis=0, concat_axis=0, tiled=True)  19.7 us
    ppermute x8, starting transfers between devices, shards(): passed = lax.ppermute(passed, 'x', far)  15.4 us
    ppermute x8, starting transfers between devices, shards(): got = lax.ppermute(send, 'x', near)  9.85 us
    all_to_all x2, starting transfers between devices, shards(): lax.all_to_all(both, ('yl', 'z'), split_axis=0, concat_axis=0, tiled=True)  9.49 us
    ppermute x6, starting transfers between devices, shards(): lax.ppermute(unit, axis, [(i, (i + by) % size) for i in range(size)])  8.67 us
    ppermute x2, waiting for transfers between devices, shards(): unit = lax.ppermute(sent, ('yh', 'c', 'x', 'yl'), to_cross)  7.48 us
    unnamed x36, local copies, waits for them, and re-layouts  5.01 us
  transfers between devices with their start and end apart: 28, of which 7 were waited for; matrix products, arithmetic and copies ran while one was open for 5% of the time, Pallas kernels for 27%

profile of v2, /device:TPU:2, one launch (start us, length us, event | category | flops | bytes accessed | tf_op | source)
XLA Modules:
  0.0 132.8 jit_solution(2423784185161896492)
XLA Ops:
  0.7 2.1 %select_bitcast_fusion.1 = (bf16[128,768]{1,0:T(8,128)(2,1)}, bf16[1,128,768]{2,1,0:T(8,128)(2,1)S(1)}, bf16[1,128,768]{2,1,0:T(8,128)(2,1)S(1)}) fusion(bf16[1,128,8192]{2,1,0:T(8,128)(2,1)} %param.8, s32[]{:T(128)S(6)} %select_n.111, bf16[1,128,8192]{2,1,0:T(8,128)(2,1)} %param.9, pred[]{:T(512)S(6)} %eq.13, s32[]{:T(128)S(6)} %select_n.109), kind=kLoop, calls=%fused_computation.25 | loop fusion | flops 98304 | bytes 1376265 | tf_op jit(solution)/shard_map/jit(_where)/select_n | solution.py:161
  3.6 3.1 %collective-permute-start.6 = (bf16[128,768]{1,0:T(8,128)(2,1)}, bf16[128,768]{1,0:T(8,128)(2,1)}, u32[]{:S(2)}, u32[]{:S(2)}) collective-permute-start(bf16[128,768]{1,0:T(8,128)(2,1)} %get-tuple-element.43), channel_id=1, source_target_pairs={{0,136},{8,128},{16,216},{24,208},{32,168},{40,160},{48,248},{56,2... | collective-permute-start | bytes 589832 | tf_op jit(solution)/shard_map/ppermute | solution.py:165
  8.0 4.3 %collective-permute-done.6.unit_0 = bf16[128,768]{1,0:T(8,128)(2,1)} collective-permute-done((bf16[128,768]{1,0:T(8,128)(2,1)}, bf16[128,768]{1,0:T(8,128)(2,1)}, u32[]{:S(2)}, u32[]{:S(2)}) %collective-permute-start.6) | collective-permute-done | bytes 196640 | tf_op jit(solution)/shard_map/ppermute | solution.py:165
  12.3 2.1 %collective-permute-start.7 = (bf16[128,768]{1,0:T(8,128)(2,1)}, bf16[128,768]{1,0:T(8,128)(2,1)S(1)}, u32[]{:S(2)}, u32[]{:S(2)}) collective-permute-start(bf16[128,768]{1,0:T(8,128)(2,1)} %collective-permute-done.6.unit_0), channel_id=1, source_target_pairs={{0,16},{16,32},{32,48},{48,0},{1,17},{17,33},{33,49},{49,1},{2,18}... | collective-permute-start | bytes 589832 | tf_op jit(solution)/shard_map/ppermute | solution.py:169
  16.0 3.2 %collective-permute-done.1.unit_0 = bf16[128,1280]{1,0:T(8,128)(2,1)S(1)} collective-permute-done((bf16[128,1280]{1,0:T(8,128)(2,1)S(1)}, bf16[128,1280]{1,0:T(8,128)(2,1)S(1)}, u32[]{:S(2)}, u32[]{:S(2)}) %collective-permute-start.1) | collective-permute-done | bytes 327712 | tf_op jit(solution)/shard_map/ppermute | solution.py:165
  19.2 1.9 %collective-permute-start.9 = (bf16[128,768]{1,0:T(8,128)(2,1)}, bf16[128,768]{1,0:T(8,128)(2,1)}, u32[]{:S(2)}, u32[]{:S(2)}) collective-permute-start(bf16[128,768]{1,0:T(8,128)(2,1)} %collective-permute-done.6.unit_0), channel_id=1, source_target_pairs={{0,1},{1,2},{2,3},{3,4},{4,5},{5,6},{6,7},{7,0},{8,9},{9,10},{10,1... | collective-permute-start | bytes 589832 | tf_op jit(solution)/shard_map/ppermute | solution.py:169
  25.3 1.9 %collective-permute-start.4 = (bf16[128,1280]{1,0:T(8,128)(2,1)S(1)}, bf16[128,1280]{1,0:T(8,128)(2,1)}, u32[]{:S(2)}, u32[]{:S(2)}) collective-permute-start(bf16[128,1280]{1,0:T(8,128)(2,1)S(1)} %collective-permute-done.1.unit_0), channel_id=1, source_target_pairs={{0,1},{1,2},{2,3},{3,4},{4,5},{5,6},{6,7},{7,0},{8,9},{9,10},{10,1... | collective-permute-start | bytes 983048 | tf_op jit(solution)/shard_map/ppermute | solution.py:169
  27.3 3.8 %collective-permute-done.9.unit_3 = bf16[128,768]{1,0:T(8,128)(2,1)} collective-permute-done((bf16[128,768]{1,0:T(8,128)(2,1)}, bf16[128,768]{1,0:T(8,128)(2,1)}, u32[]{:S(2)}, u32[]{:S(2)}) %collective-permute-start.9) | collective-permute-done | bytes 196640 | tf_op jit(solution)/shard_map/ppermute | solution.py:169
  34.0 12.2 %attention.4 = (bf16[640,2048]{1,0:T(8,128)(2,1)}, bf16[256,768]{1,0:T(8,128)(2,1)S(1)}, bf16[256,768]{1,0:T(8,128)(2,1)S(1)}, bf16[256,768]{1,0:T(8,128)(2,1)S(1)}, bf16[256,768]{1,0:T(8,128)(2,1)S(1)}) custom-call(s32[17]{0:T(128)S(1)} %stack.84.place, s32[8]{0:T(128)S(1)} %bitcast.62, f32[16]{0:T(128)S(1)} %tanh_bitcast_fusion.factor, ...), custom_call_target="tpu_custom_call" | custom-call | flops 2516582400 | bytes 6291456 | tf_op jit(solution)/shard_map/attention/pallas_call | solution.py:97
  46.2 2.7 %collective-permute-start.12 = (bf16[256,768]{1,0:T(8,128)(2,1)S(1)}, bf16[256,768]{1,0:T(8,128)(2,1)S(1)}, u32[]{:S(2)}, u32[]{:S(2)}) collective-permute-start(bf16[256,768]{1,0:T(8,128)(2,1)S(1)} %get-tuple-element.30), channel_id=1, source_target_pairs={{0,48},{16,32},{32,16},{48,0},{1,49},{17,33},{33,17},{49,1},{2,50}... | collective-permute-start | bytes 1179656 | tf_op jit(solution)/shard_map/ppermute | solution.py:189
  48.9 8.9 %attention.5 = (bf16[640,2048]{1,0:T(8,128)(2,1)}, bf16[256,512]{1,0:T(8,128)(2,1)S(1)}, bf16[256,512]{1,0:T(8,128)(2,1)S(1)}, bf16[256,512]{1,0:T(8,128)(2,1)S(1)}, bf16[256,512]{1,0:T(8,128)(2,1)S(1)}) custom-call(s32[17]{0:T(128)S(1)} %stack.84.place, s32[8]{0:T(128)S(1)} %bitcast.63, ...), custom_call_target="tpu_custom_call", output_to_operand_aliasing={{0}: (14, {})} | custom-call | flops 1677721600 | bytes 4194304 | tf_op jit(solution)/shard_map/attention/pallas_call | solution.py:97
  60.0 7.1 %attention.6 = (bf16[640,2048]{1,0:T(8,128)(2,1)}, bf16[256,384]{1,0:T(8,128)(2,1)S(1)}, bf16[256,384]{1,0:T(8,128)(2,1)S(1)}, bf16[256,384]{1,0:T(8,128)(2,1)S(1)}, bf16[256,384]{1,0:T(8,128)(2,1)S(1)}) custom-call(s32[17]{0:T(128)S(1)} %stack.84.place, s32[8]{0:T(128)S(1)} %bitcast.64, ...), custom_call_target="tpu_custom_call", output_to_operand_aliasing={{0}: (14, {})} | custom-call | flops 1258291200 | bytes 3145728 | tf_op jit(solution)/shard_map/attention/pallas_call | solution.py:97
  67.8 7.1 %attention.7 = (bf16[640,2048]{1,0:T(8,128)(2,1)}, bf16[256,384]{1,0:T(8,128)(2,1)S(1)}, bf16[256,384]{1,0:T(8,128)(2,1)S(1)}, bf16[256,384]{1,0:T(8,128)(2,1)S(1)}, bf16[256,384]{1,0:T(8,128)(2,1)S(1)}) custom-call(s32[17]{0:T(128)S(1)} %stack.84.place, s32[8]{0:T(128)S(1)} %bitcast.65, ...), custom_call_target="tpu_custom_call", output_to_operand_aliasing={{0}: (14, {})} | custom-call | flops 1258291200 | bytes 3145728 | tf_op jit(solution)/shard_map/attention/pallas_call | solution.py:97
  74.9 2.1 %collective-permute-start.20 = (bf16[256,384]{1,0:T(8,128)(2,1)S(1)}, bf16[256,384]{1,0:T(8,128)(2,1)S(1)}, u32[]{:S(2)}, u32[]{:S(2)}) collective-permute-start(bf16[256,384]{1,0:T(8,128)(2,1)S(1)} %get-tuple-element.38), channel_id=1, source_target_pairs={{0,48},{16,32},{32,16},{48,0},{1,49},{17,33},{33,17},{49,1},{2,50}... | collective-permute-start | bytes 589832 | tf_op jit(solution)/shard_map/ppermute | solution.py:189
  79.3 3.5 %collective-permute-done.20 = bf16[256,384]{1,0:T(8,128)(2,1)S(1)} collective-permute-done((bf16[256,384]{1,0:T(8,128)(2,1)S(1)}, bf16[256,384]{1,0:T(8,128)(2,1)S(1)}, u32[]{:S(2)}, u32[]{:S(2)}) %collective-permute-start.20) | collective-permute-done | bytes 196640 | tf_op jit(solution)/shard_map/ppermute | solution.py:189
  82.8 2.0 %collective-permute-start.11 = (bf16[128,768]{1,0:T(8,128)(2,1)S(1)}, bf16[128,768]{1,0:T(8,128)(2,1)S(1)}, u32[]{:S(2)}, u32[]{:S(2)}) collective-permute-start(bf16[128,768]{1,0:T(8,128)(2,1)S(1)} %add_convert_fusion.3), channel_id=1, source_target_pairs={{0,48},{16,32},{32,16},{48,0},{1,49},{17,33},{33,17},{49,1},{2,50}... | collective-permute-start | bytes 589832 | tf_op jit(solution)/shard_map/ppermute | solution.py:191
  84.8 2.0 %collective-permute-start.13 = (bf16[128,768]{1,0:T(8,128)(2,1)S(1)}, bf16[128,768]{1,0:T(8,128)(2,1)S(1)}, u32[]{:S(2)}, u32[]{:S(2)}) collective-permute-start(bf16[128,768]{1,0:T(8,128)(2,1)S(1)} %add_convert_fusion.1), channel_id=1, source_target_pairs={{0,16},{16,0},{32,48},{48,32},{1,17},{17,1},{33,49},{49,33},{2,18}... | collective-permute-start | bytes 589832 | tf_op jit(solution)/shard_map/ppermute | solution.py:191
  87.0 2.0 %collective-permute-start.19 = (bf16[128,384]{1,0:T(8,128)(2,1)S(1)}, bf16[128,384]{1,0:T(8,128)(2,1)S(1)}, u32[]{:S(2)}, u32[]{:S(2)}) collective-permute-start(bf16[128,384]{1,0:T(8,128)(2,1)S(1)} %add_convert_fusion.15), channel_id=1, source_target_pairs={{0,48},{16,32},{32,16},{48,0},{1,49},{17,33},{33,17},{49,1},{2,50}... | collective-permute-start | bytes 294920 | tf_op jit(solution)/shard_map/ppermute | solution.py:191
  89.0 2.0 %collective-permute-start.21 = (bf16[128,384]{1,0:T(8,128)(2,1)S(1)}, bf16[128,384]{1,0:T(8,128)(2,1)S(1)}, u32[]{:S(2)}, u32[]{:S(2)}) collective-permute-start(bf16[128,384]{1,0:T(8,128)(2,1)S(1)} %add_convert_fusion.13), channel_id=1, source_target_pairs={{0,16},{16,0},{32,48},{48,32},{1,17},{17,1},{33,49},{49,33},{2,18}... | collective-permute-start | bytes 294920 | tf_op jit(solution)/shard_map/ppermute | solution.py:191
  92.5 3.9 %collective-permute-start.25 = (bf16[128,384]{1,0:T(8,128)(2,1)S(1)}, bf16[128,384]{1,0:T(8,128)(2,1)S(1)}, u32[]{:S(2)}, u32[]{:S(2)}) collective-permute-start(bf16[128,384]{1,0:T(8,128)(2,1)S(1)} %add_convert_fusion.9), channel_id=1, source_target_pairs={{0,16},{16,0},{32,48},{48,32},{1,17},{17,1},{33,49},{49,33},{2,18}... | collective-permute-start | bytes 294920 | tf_op jit(solution)/shard_map/ppermute | solution.py:191
  99.8 5.2 %all-to-all-start = ((bf16[16,2,8,768]{3,2,1,0:T(8,128)(2,1)}), bf16[16,2,8,768]{3,2,1,0:T(8,128)(2,1)S(1)}, u32[]{:S(2)}, u32[]{:S(2)}) async-start(bf16[16,2,8,768]{3,2,1,0:T(8,128)(2,1)} %pad_maximum_fusion.2), calls=%async_computation | async-start | bytes 786432 | tf_op jit(solution)/shard_map/all_to_all | solution.py:198
  107.9 7.4 %all-to-all-done = bf16[16,2,8,768]{3,2,1,0:T(8,128)(2,1)S(1)} async-done(((bf16[16,2,8,768]{3,2,1,0:T(8,128)(2,1)}), bf16[16,2,8,768]{3,2,1,0:T(8,128)(2,1)S(1)}, u32[]{:S(2)}, u32[]{:S(2)}) %all-to-all-start) | async-done | bytes 393248 | tf_op jit(solution)/shard_map/all_to_all | solution.py:198
  115.3 4.3 %all-to-all-start.1 = ((bf16[16,2,8,1280]{3,2,1,0:T(8,128)(2,1)}), bf16[16,2,8,1280]{3,2,1,0:T(8,128)(2,1)S(1)}, u32[]{:S(2)}, u32[]{:S(2)}) async-start(bf16[16,2,8,1280]{3,2,1,0:T(8,128)(2,1)} %maximum_maximum_fusion), calls=%async_computation.1 | async-start | bytes 1310720 | tf_op jit(solution)/shard_map/all_to_all | solution.py:198
  119.7 12.4 %all-to-all-done.1 = bf16[16,2,8,1280]{3,2,1,0:T(8,128)(2,1)S(1)} async-done(((bf16[16,2,8,1280]{3,2,1,0:T(8,128)(2,1)}), bf16[16,2,8,1280]{3,2,1,0:T(8,128)(2,1)S(1)}, u32[]{:S(2)}, u32[]{:S(2)}) %all-to-all-start.1) | async-done | bytes 655392 | tf_op jit(solution)/shard_map/all_to_all | solution.py:198
  (100 shorter events, 24.8 us)
Async XLA Ops:
  3.6 17.5 %collective-permute-start.5 = (bf16[2,128,768]{2,1,0:T(8,128)(2,1)}, bf16[2,128,768]{2,1,0:T(8,128)(2,1)S(1)}, u32[]{:S(2)}, u32[]{:S(2)}) collective-permute-start(bf16[2,128,768]{2,1,0:T(8,128)(2,1)} %pad_maximum_fusion.1), channel_id=1, source_target_pairs={{0,64},{64,0},{1,65},{65,1},{2,66},{66,2},{3,67},{67,3},{4,68},{68... | collective-permute-start | bytes 1179656 | tf_op jit(solution)/shard_map/ppermute | solution.py:166
  3.6 8.7 %collective-permute-start.6 = (bf16[128,768]{1,0:T(8,128)(2,1)}, bf16[128,768]{1,0:T(8,128)(2,1)}, u32[]{:S(2)}, u32[]{:S(2)}) collective-permute-start(bf16[128,768]{1,0:T(8,128)(2,1)} %get-tuple-element.43), channel_id=1, source_target_pairs={{0,136},{8,128},{16,216},{24,208},{32,168},{40,160},{48,248},{56,2... | collective-permute-start | bytes 589832 | tf_op jit(solution)/shard_map/ppermute | solution.py:165
  7.9 11.3 %collective-permute-start.1 = (bf16[128,1280]{1,0:T(8,128)(2,1)S(1)}, bf16[128,1280]{1,0:T(8,128)(2,1)S(1)}, u32[]{:S(2)}, u32[]{:S(2)}) collective-permute-start(bf16[128,1280]{1,0:T(8,128)(2,1)S(1)} %get-tuple-element.46), channel_id=1, source_target_pairs={{0,136},{8,128},{16,216},{24,208},{32,168},{40,160},{48,248},{56,2... | collective-permute-start | bytes 983048 | tf_op jit(solution)/shard_map/ppermute | solution.py:165
  12.3 11.2 %collective-permute-start.7 = (bf16[128,768]{1,0:T(8,128)(2,1)}, bf16[128,768]{1,0:T(8,128)(2,1)S(1)}, u32[]{:S(2)}, u32[]{:S(2)}) collective-permute-start(bf16[128,768]{1,0:T(8,128)(2,1)} %collective-permute-done.6.unit_0), channel_id=1, source_target_pairs={{0,16},{16,32},{32,48},{48,0},{1,17},{17,33},{33,49},{49,1},{2,18}... | collective-permute-start | bytes 589832 | tf_op jit(solution)/shard_map/ppermute | solution.py:169
  14.4 10.2 %collective-permute-start.8 = (bf16[128,768]{1,0:T(8,128)(2,1)}, bf16[128,768]{1,0:T(8,128)(2,1)S(1)}, u32[]{:S(2)}, u32[]{:S(2)}) collective-permute-start(bf16[128,768]{1,0:T(8,128)(2,1)} %collective-permute-done.6.unit_0), channel_id=1, source_target_pairs={{0,48},{16,0},{32,16},{48,32},{1,49},{17,1},{33,17},{49,33},{2,50}... | collective-permute-start | bytes 589832 | tf_op jit(solution)/shard_map/ppermute | solution.py:169
  16.0 30.1 %collective-permute-start = (bf16[2,128,1280]{2,1,0:T(8,128)(2,1)}, bf16[2,128,1280]{2,1,0:T(8,128)(2,1)S(1)}, u32[]{:S(2)}, u32[]{:S(2)}) collective-permute-start(bf16[2,128,1280]{2,1,0:T(8,128)(2,1)} %pad_maximum_fusion), channel_id=1, source_target_pairs={{0,64},{64,0},{1,65},{65,1},{2,66},{66,2},{3,67},{67,3},{4,68},{68... | collective-permute-start | bytes 1966088 | tf_op jit(solution)/shard_map/ppermute | solution.py:166
  19.2 11.9 %collective-permute-start.9 = (bf16[128,768]{1,0:T(8,128)(2,1)}, bf16[128,768]{1,0:T(8,128)(2,1)}, u32[]{:S(2)}, u32[]{:S(2)}) collective-permute-start(bf16[128,768]{1,0:T(8,128)(2,1)} %collective-permute-done.6.unit_0), channel_id=1, source_target_pairs={{0,1},{1,2},{2,3},{3,4},{4,5},{5,6},{6,7},{7,0},{8,9},{9,10},{10,1... | collective-permute-start | bytes 589832 | tf_op jit(solution)/shard_map/ppermute | solution.py:169
  21.9 27.0 %collective-permute-start.2 = (bf16[128,1280]{1,0:T(8,128)(2,1)S(1)}, bf16[128,1280]{1,0:T(8,128)(2,1)S(1)}, u32[]{:S(2)}, u32[]{:S(2)}) collective-permute-start(bf16[128,1280]{1,0:T(8,128)(2,1)S(1)} %collective-permute-done.1.unit_0), channel_id=1, source_target_pairs={{0,16},{16,32},{32,48},{48,0},{1,17},{17,33},{33,49},{49,1},{2,18}... | collective-permute-start | bytes 983048 | tf_op jit(solution)/shard_map/ppermute | solution.py:169
  24.2 24.6 %collective-permute-start.3 = (bf16[128,1280]{1,0:T(8,128)(2,1)S(1)}, bf16[128,1280]{1,0:T(8,128)(2,1)}, u32[]{:S(2)}, u32[]{:S(2)}) collective-permute-start(bf16[128,1280]{1,0:T(8,128)(2,1)S(1)} %collective-permute-done.1.unit_0), channel_id=1, source_target_pairs={{0,48},{16,0},{32,16},{48,32},{1,49},{17,1},{33,17},{49,33},{2,50}... | collective-permute-start | bytes 983048 | tf_op jit(solution)/shard_map/ppermute | solution.py:169
  25.3 23.6 %collective-permute-start.4 = (bf16[128,1280]{1,0:T(8,128)(2,1)S(1)}, bf16[128,1280]{1,0:T(8,128)(2,1)}, u32[]{:S(2)}, u32[]{:S(2)}) collective-permute-start(bf16[128,1280]{1,0:T(8,128)(2,1)S(1)} %collective-permute-done.1.unit_0), channel_id=1, source_target_pairs={{0,1},{1,2},{2,3},{3,4},{4,5},{5,6},{6,7},{7,0},{8,9},{9,10},{10,1... | collective-permute-start | bytes 983048 | tf_op jit(solution)/shard_map/ppermute | solution.py:169
  46.2 28.8 %collective-permute-start.10 = (bf16[256,768]{1,0:T(8,128)(2,1)S(1)}, bf16[256,768]{1,0:T(8,128)(2,1)S(1)}, u32[]{:S(2)}, u32[]{:S(2)}) collective-permute-start(bf16[256,768]{1,0:T(8,128)(2,1)S(1)} %get-tuple-element.28), channel_id=1, source_target_pairs={{0,16},{16,0},{32,48},{48,32},{1,17},{17,1},{33,49},{49,33},{2,18}... | collective-permute-start | bytes 1179656 | tf_op jit(solution)/shard_map/ppermute | solution.py:189
  46.2 30.9 %collective-permute-start.12 = (bf16[256,768]{1,0:T(8,128)(2,1)S(1)}, bf16[256,768]{1,0:T(8,128)(2,1)S(1)}, u32[]{:S(2)}, u32[]{:S(2)}) collective-permute-start(bf16[256,768]{1,0:T(8,128)(2,1)S(1)} %get-tuple-element.30), channel_id=1, source_target_pairs={{0,48},{16,32},{32,16},{48,0},{1,49},{17,33},{33,17},{49,1},{2,50}... | collective-permute-start | bytes 1179656 | tf_op jit(solution)/shard_map/ppermute | solution.py:189
  57.7 31.3 %collective-permute-start.14 = (bf16[256,512]{1,0:T(8,128)(2,1)S(1)}, bf16[256,512]{1,0:T(8,128)(2,1)S(1)}, u32[]{:S(2)}, u32[]{:S(2)}) collective-permute-start(bf16[256,512]{1,0:T(8,128)(2,1)S(1)} %get-tuple-element.32), channel_id=1, source_target_pairs={{0,16},{16,0},{32,48},{48,32},{1,17},{17,1},{33,49},{49,33},{2,18}... | collective-permute-start | bytes 786440 | tf_op jit(solution)/shard_map/ppermute | solution.py:189
  59.5 31.6 %collective-permute-start.16 = (bf16[256,512]{1,0:T(8,128)(2,1)S(1)}, bf16[256,512]{1,0:T(8,128)(2,1)S(1)}, u32[]{:S(2)}, u32[]{:S(2)}) collective-permute-start(bf16[256,512]{1,0:T(8,128)(2,1)S(1)} %get-tuple-element.34), channel_id=1, source_target_pairs={{0,48},{16,32},{32,16},{48,0},{1,49},{17,33},{33,17},{49,1},{2,50}... | collective-permute-start | bytes 786440 | tf_op jit(solution)/shard_map/ppermute | solution.py:189
  67.1 11.6 %collective-permute-start.18 = (bf16[256,384]{1,0:T(8,128)(2,1)S(1)}, bf16[256,384]{1,0:T(8,128)(2,1)S(1)}, u32[]{:S(2)}, u32[]{:S(2)}) collective-permute-start(bf16[256,384]{1,0:T(8,128)(2,1)S(1)} %get-tuple-element.36), channel_id=1, source_target_pairs={{0,16},{16,0},{32,48},{48,32},{1,17},{17,1},{33,49},{49,33},{2,18}... | collective-permute-start | bytes 589832 | tf_op jit(solution)/shard_map/ppermute | solution.py:189
  74.9 7.9 %collective-permute-start.20 = (bf16[256,384]{1,0:T(8,128)(2,1)S(1)}, bf16[256,384]{1,0:T(8,128)(2,1)S(1)}, u32[]{:S(2)}, u32[]{:S(2)}) collective-permute-start(bf16[256,384]{1,0:T(8,128)(2,1)S(1)} %get-tuple-element.38), channel_id=1, source_target_pairs={{0,48},{16,32},{32,16},{48,0},{1,49},{17,33},{33,17},{49,1},{2,50}... | collective-permute-start | bytes 589832 | tf_op jit(solution)/shard_map/ppermute | solution.py:189
  78.7 8.3 %collective-permute-start.24 = (bf16[256,384]{1,0:T(8,128)(2,1)S(1)}, bf16[256,384]{1,0:T(8,128)(2,1)S(1)}, u32[]{:S(2)}, u32[]{:S(2)}) collective-permute-start(bf16[256,384]{1,0:T(8,128)(2,1)S(1)} %get-tuple-element.42), channel_id=1, source_target_pairs={{0,48},{16,32},{32,16},{48,0},{1,49},{17,33},{33,17},{49,1},{2,50}... | collective-permute-start | bytes 589832 | tf_op jit(solution)/shard_map/ppermute | solution.py:189
  82.8 16.0 %collective-permute-start.11 = (bf16[128,768]{1,0:T(8,128)(2,1)S(1)}, bf16[128,768]{1,0:T(8,128)(2,1)S(1)}, u32[]{:S(2)}, u32[]{:S(2)}) collective-permute-start(bf16[128,768]{1,0:T(8,128)(2,1)S(1)} %add_convert_fusion.3), channel_id=1, source_target_pairs={{0,48},{16,32},{32,16},{48,0},{1,49},{17,33},{33,17},{49,1},{2,50}... | collective-permute-start | bytes 589832 | tf_op jit(solution)/shard_map/ppermute | solution.py:191
  84.8 14.1 %collective-permute-start.13 = (bf16[128,768]{1,0:T(8,128)(2,1)S(1)}, bf16[128,768]{1,0:T(8,128)(2,1)S(1)}, u32[]{:S(2)}, u32[]{:S(2)}) collective-permute-start(bf16[128,768]{1,0:T(8,128)(2,1)S(1)} %add_convert_fusion.1), channel_id=1, source_target_pairs={{0,16},{16,0},{32,48},{48,32},{1,17},{17,1},{33,49},{49,33},{2,18}... | collective-permute-start | bytes 589832 | tf_op jit(solution)/shard_map/ppermute | solution.py:191
  92.5 12.5 %collective-permute-start.25 = (bf16[128,384]{1,0:T(8,128)(2,1)S(1)}, bf16[128,384]{1,0:T(8,128)(2,1)S(1)}, u32[]{:S(2)}, u32[]{:S(2)}) collective-permute-start(bf16[128,384]{1,0:T(8,128)(2,1)S(1)} %add_convert_fusion.9), channel_id=1, source_target_pairs={{0,16},{16,0},{32,48},{48,32},{1,17},{17,1},{33,49},{49,33},{2,18}... | collective-permute-start | bytes 294920 | tf_op jit(solution)/shard_map/ppermute | solution.py:191
  96.5 8.6 %collective-permute-start.15 = (bf16[128,512]{1,0:T(8,128)(2,1)S(1)}, bf16[128,512]{1,0:T(8,128)(2,1)S(1)}, u32[]{:S(2)}, u32[]{:S(2)}) collective-permute-start(bf16[128,512]{1,0:T(8,128)(2,1)S(1)} %add_convert_fusion.7), channel_id=1, source_target_pairs={{0,48},{16,32},{32,16},{48,0},{1,49},{17,33},{33,17},{49,1},{2,50}... | collective-permute-start | bytes 393224 | tf_op jit(solution)/shard_map/ppermute | solution.py:191
  97.3 8.7 %collective-permute-start.17 = (bf16[128,512]{1,0:T(8,128)(2,1)S(1)}, bf16[128,512]{1,0:T(8,128)(2,1)S(1)}, u32[]{:S(2)}, u32[]{:S(2)}) collective-permute-start(bf16[128,512]{1,0:T(8,128)(2,1)S(1)} %add_convert_fusion.5), channel_id=1, source_target_pairs={{0,16},{16,0},{32,48},{48,32},{1,17},{17,1},{33,49},{49,33},{2,18}... | collective-permute-start | bytes 393224 | tf_op jit(solution)/shard_map/ppermute | solution.py:191
  99.8 15.5 %all-to-all-start = ((bf16[16,2,8,768]{3,2,1,0:T(8,128)(2,1)}), bf16[16,2,8,768]{3,2,1,0:T(8,128)(2,1)S(1)}, u32[]{:S(2)}, u32[]{:S(2)}) async-start(bf16[16,2,8,768]{3,2,1,0:T(8,128)(2,1)} %pad_maximum_fusion.2), calls=%async_computation | async-start | bytes 786432 | tf_op jit(solution)/shard_map/all_to_all | solution.py:198
  115.3 16.8 %all-to-all-start.1 = ((bf16[16,2,8,1280]{3,2,1,0:T(8,128)(2,1)}), bf16[16,2,8,1280]{3,2,1,0:T(8,128)(2,1)S(1)}, u32[]{:S(2)}, u32[]{:S(2)}) async-start(bf16[16,2,8,1280]{3,2,1,0:T(8,128)(2,1)} %maximum_maximum_fusion), calls=%async_computation.1 | async-start | bytes 1310720 | tf_op jit(solution)/shard_map/all_to_all | solution.py:198
  (22 other events, 245.3 us)

commit v3 on v2

v3 whole, which is shorter than its diff:
```python
import functools
import math

import jax
import jax.numpy as jnp
from jax import lax
from jax.experimental import pallas as pl
from jax.experimental.pallas import tpu as pltpu
from jax.sharding import Mesh, PartitionSpec as P


HEAD = 128
NT = (((1,), (1,)), ((), ()))
NN = (((1,), (0,)), ((), ()))
TN = (((0,), (0,)), ((), ()))
LOG2E = math.log2(math.e)
SCALE = 1.0 / math.sqrt(HEAD)
GATHERS = ((8,), (8,))
PLANES = ((0,), (1,))
AXES = ("yh", "c", "x", "yl", "z")


def score_stage(query, grad_in, keys, values, factor):
    gated = (grad_in.astype(jnp.float32) * factor).astype(jnp.bfloat16)
    scores = lax.dot_general(keys, query, NT, preferred_element_type=jnp.float32)
    weight_grad = lax.dot_general(values, gated, NT, preferred_element_type=jnp.float32)
    return scores, weight_grad, gated


def by_eights(op, blocks):
    folded = [op(b.reshape(-1, 8, b.shape[1]), axis=0) for b in blocks]
    return functools.reduce(jnp.maximum if op is jnp.max else jnp.add, folded)


def weight_stage(scores, weight_grad, allowed, scale):
    block = scores.shape[0] // len(allowed)
    cut = lambda array: [array[b * block : (b + 1) * block] for b in range(len(allowed))]
    masked = [jnp.where(a, s, -1e30) for a, s in zip(allowed, cut(scores))]
    grads = cut(weight_grad)
    top = jnp.max(by_eights(jnp.max, masked), axis=0, keepdims=True)
    exponent = [jnp.exp2((m - top) * (scale * LOG2E)) for m in masked]
    share = 1.0 / jnp.sum(by_eights(jnp.sum, exponent), axis=0, keepdims=True)
    crossed = by_eights(jnp.sum, [e * g for e, g in zip(exponent, grads)])
    row_delta = jnp.sum(crossed, axis=0, keepdims=True) * share
    weights = [e * share for e in exponent]
    weights_half = jnp.concatenate([w.astype(jnp.bfloat16) for w in weights], axis=0)
    score_half = jnp.concatenate(
        [(w * (g - row_delta)).astype(jnp.bfloat16) for w, g in zip(weights, grads)], axis=0
    )
    return weights_half, score_half


def attention_body(
    place, order, factor, seen, query, grad_in, key_own, value_own, key_pair, value_pair,
    unit_0, unit_1, unit_2, unit_3, *rest, first, scale, step,
):
    query_out, key_send, key_keep, value_send, value_keep, latents = rest[-6:]
    head = first + pl.program_id(0) * step
    sources = (key_own, value_own, key_pair, value_pair, unit_0, unit_1, unit_2, unit_3)
    for i, source in enumerate(sources):
        latents[pl.ds(pl.multiple_of(place[1 + i], 128), 128), :] = source[...].reshape(128, step * HEAD)
    allowed = [order[place[9 + b]] < seen[...] for b in range(8)]
    total = latents.shape[0] // 2
    at = [slice(i * HEAD, (i + 1) * HEAD) for i in range(step)]
    scored, weighed = [None] * step, [None] * step

    def score(i):
        scored[i] = score_stage(
            query[:, at[i]], grad_in[:, at[i]], latents[:total, at[i]], latents[total:, at[i]], factor[head + i]
        )

    def weigh(i):
        weighed[i] = weight_stage(scored[i][0], scored[i][1], allowed, scale)

    def project(i):
        weights_half, score_half = weighed[i]
        dot = lambda a, b, dims: lax.dot_general(a, b, dims, preferred_element_type=jnp.float32)
        query_part = dot(latents[:total, at[i]], score_half, TN) * scale
        query_out[:, at[i]] = jnp.transpose(query_part).astype(jnp.bfloat16)
        key_part = dot(score_half, query[:, at[i]], NN).astype(jnp.bfloat16)
        key_send[:, at[i]] = key_part[:256]
        key_keep[:, at[i]] = key_part[256:]
        value_part = dot(weights_half, scored[i][2], NN).astype(jnp.bfloat16)
        for slot, (out, row) in enumerate(((value_send, 0), (value_keep, 0), (value_send, 128), (value_keep, 128))):
            out[row : row + 128, at[i]] = value_part[slot * 128 : (slot + 1) * 128]

    score(0)
    for i in range(step):
        if i + 1 < step:
            score(i + 1)
        weigh(i)
        if i:
            project(i - 1)
    project(step - 1)


def attention(place, order, factor, seen, query, grad_in, key_own, value_own, pair, units, buffer, first, count, offset):
    tokens = query.shape[0]
    step = next(s for s in (4, 3, 2, 1) if count % s == first % s == offset % s == 0)
    width = step * HEAD
    scalar = pl.BlockSpec(memory_space=pltpu.SMEM)
    head_of = lambda h, place: (0, first // step + h)
    own_of = lambda h, place: (0, place[0] // step + first // step + h)
    part = lambda rows, at=0: pl.BlockSpec((rows, width), lambda h, place: (0, at // step + h))
    paired = lambda which: pl.BlockSpec((1, 128, width), lambda h, place: (which, 0, offset // step + h))
    grads = jax.ShapeDtypeStruct((256, count * HEAD), jnp.bfloat16)
    grid_spec = pltpu.PrefetchScalarGridSpec(
        num_scalar_prefetch=1,
        grid=(count // step,),
        in_specs=[
            scalar,
            scalar,
            pl.BlockSpec((1, tokens), lambda h, place: (0, 0)),
            pl.BlockSpec((tokens, width), head_of),
            pl.BlockSpec((tokens, width), head_of),
            pl.BlockSpec((128, width), own_of),
            pl.BlockSpec((128, width), own_of),
            paired(0),
            paired(1),
        ]
        + [part(128, offset)] * 4
        + [pl.BlockSpec(memory_space=pl.ANY)] * len(buffer),
        out_specs=[pl.BlockSpec((tokens, width), head_of)] + [part(256)] * 4,
        scratch_shapes=[pltpu.VMEM((1024, width), jnp.bfloat16)],
    )
    matmul = 2 * tokens * 512 * HEAD
    return pl.pallas_call(
        functools.partial(attention_body, first=first, scale=SCALE, step=step),
        grid_spec=grid_spec,
        out_shape=[jax.ShapeDtypeStruct(query.shape, jnp.bfloat16)] + [grads] * 4,
        input_output_aliases={14: 0} if buffer else {},
        compiler_params=pltpu.CompilerParams(dimension_semantics=("arbitrary",), vmem_limit_bytes=48 * 2**20),
        cost_estimate=pl.CostEstimate(
            flops=5 * count * matmul, transcendentals=count * tokens * 512, bytes_accessed=count * 2**20
        ),
        name="attention",
    )(place, order, factor, seen, query, grad_in, key_own, value_own, pair, pair, *units, *buffer)


def relabel(sizes, move):
    pairs = []
    total = math.prod(sizes)
    for source in range(total):
        rest, at = source, []
        for size in reversed(sizes):
            at.append(rest % size)
            rest //= size
        to = 0
        for index, size in zip(move(*reversed(at)), sizes):
            to = to * size + index % size
        pairs.append((source, to))
    return pairs


def columns(array, start, width):
    return lax.dynamic_slice(array, (0, start), (array.shape[0], width))


def shards(queries, visual_keys, visual_values, out_grad, gate_value, image_order, image_seen):
    query, grad_in, keys, values = queries[0], out_grad[0], visual_keys[0], visual_values[0]
    local = query.shape[1]
    heads = local // HEAD
    yh, c, x, _, z = (lax.axis_index(a) for a in AXES)
    colour = lambda x, z, c: (x + 2 * z) % 4 ^ c
    slot = lambda owner: 135 >> 2 * (owner ^ x) & 3
    row_block = lambda owner: slot(owner) * 128
    unit_at = lambda unit: unit // 2 * 512 + row_block((1 - yh) * 2 + unit % 2)
    own = yh * 2 + c
    pair_owner = yh * 2 + 1 - c
    place = [own * heads, row_block(own), 512 + row_block(own), row_block(pair_owner), 512 + row_block(pair_owner)]
    place += [unit_at(colour(x + dx, z + dz, c)) for dx, dz in ((0, 0), (3, 0), (1, 0), (0, 7))]
    place += [(x ^ flip) * 2 + half for flip in (2, 1, 3, 0) for half in (0, 1)]
    place = jnp.stack(place).astype(jnp.int32)
    factor = jnp.tanh(gate_value[0])
    seen = image_seen[None]

    to_cross = relabel((2, 2, 4, 2), lambda yh, c, x, yl: (1 - yh, c ^ (x & 1), x, 1 - yl))
    flip_pairs = [(i, i ^ 1) for i in range(4)]
    cross_pairs = [(i, 3 - i) for i in range(4)]
    there = (1 - yh) * 2 + (c ^ (x & 1))
    wants_values = (x + 2 * z) % 4 // 2 == 1

    gathered = []
    first = 0
    for counts in GATHERS:
        at, width = first * HEAD, sum(counts) * HEAD
        sent = jnp.where(
            wants_values, columns(values, there * local + at, width), columns(keys, there * local + at, width)
        )
        pair = jnp.stack([columns(a, pair_owner * local + at, width) for a in (keys, values)])
        unit = lax.ppermute(sent, ("yh", "c", "x", "yl"), to_cross)
        pair = lax.ppermute(pair, "c", [(0, 1), (1, 0)])
        units = [unit]
        for axis, size, by in (("x", 4, 1), ("x", 4, 3), ("z", 8, 1)):
            units.append(lax.ppermute(unit, axis, [(i, (i + by) % size) for i in range(size)]))
        offset = 0
        for count in counts:
            gathered.append((pair, units, first, count, offset))
            first += count
            offset += count

    buffer = ()
    ready, parts = [], []
    f32 = jnp.float32
    for pair, units, first, count, offset in gathered:
        whole, key_send, key_keep, value_send, value_keep = attention(
            place, image_order[0], factor, seen, query, grad_in, keys, values, pair, units,
            buffer, first, count, offset,
        )
        buffer = (whole,)
        mine = []
        for send, keep, near, far in (
            (key_send, key_keep, flip_pairs, cross_pairs), (value_send, value_keep, cross_pairs, flip_pairs)
        ):
            got = lax.ppermute(send, "x", near)
            passed = (keep[:128].astype(f32) + got[:128].astype(f32)).astype(jnp.bfloat16)
            passed = lax.ppermute(passed, "x", far)
            mine.append(
                (keep[128:].astype(f32) + got[128:].astype(f32) + passed.astype(f32)).astype(jnp.bfloat16)
            )
        ready.append(jnp.stack([m.reshape(16, 8, count * HEAD) for m in mine], axis=1))
    for members in PLANES:
        both = jnp.concatenate([ready[m] for m in members], axis=3)
        arrived = lax.all_to_all(both, ("yl", "z"), split_axis=0, concat_axis=0, tiled=True)
        parts.append(arrived.astype(f32).sum(axis=0))
    result = jnp.concatenate(parts, axis=2)
    return whole[None], result[0][None] * SCALE, result[1][None]


def solution(mesh):
    torus = Mesh(mesh.devices.reshape(2, 2, 4, 2, 8), AXES)
    img, txt = ("yh", "c"), ("x", "yl", "z")
    placed = (
        P(None, txt, img),
        P(None, img, None),
        P(None, img, None),
        P(None, txt, img),
        P(None, img),
        P(),
        P(txt),
    )
    return jax.shard_map(shards, mesh=torus, in_specs=placed, out_specs=(P(None, txt, img),) * 3, check_vma=False)
```

time: 135 us -> 119 us (0.88)
  waiting for transfers between devices: 34.8 us -> 50.2 us
  starting transfers between devices: 46.6 us -> 35.2 us
  Pallas kernels: 35.3 us -> 24.4 us
  local copies, waits for them, and re-layouts: 5.11 us -> 0.13 us
  other arithmetic: 9.95 us -> 6.94 us
    ppermute x6, waiting for transfers between devices: 3.81 us -> 15.6 us  [shards(): lax.ppermute(unit, axis, [(i, (i + by) % size) for i in range(size)])]
    pallas_call x4 -> x2, Pallas kernels: 35.3 us -> 24.4 us  [attention(): pl.pallas_call(functools.partial(attention_body, first=first, scale=SCALE...]
    ppermute x8 -> x4, starting transfers between devices: 15.4 us -> 6.81 us  [shards(): passed = lax.ppermute(passed, 'x', far)]
    unnamed x36 -> x14, local copies, waits for them, and re-layouts: 5.01 us -> 0.03 us
    all_to_all x2, waiting for transfers between devices: 19.7 us -> 14.8 us  [shards(): lax.all_to_all(both, ('yl', 'z'), split_axis=0, concat_axis=0, tiled=True)]
    ppermute x8 -> x4, starting transfers between devices: 9.85 us -> 4.95 us  [shards(): got = lax.ppermute(send, 'x', near)]
    ppermute x8 -> x4, waiting for transfers between devices: 0.02 us -> 4.55 us  [shards(): passed = lax.ppermute(passed, 'x', far)]
    ppermute x2, waiting for transfers between devices: 7.48 us -> 11.1 us  [shards(): unit = lax.ppermute(sent, ('yh', 'c', 'x', 'yl'), to_cross)]
  transfers between devices with their start and end apart: 28 -> 20, of which waited for: 7 -> 14; matrix products, arithmetic and copies ran while one was open for 5% -> 3% of each run, Pallas kernels for 27% -> 10%
where the time goes in v3:
time: 119 us; the launch traced here: 118 us
  waiting for transfers between devices  50.2 us (42%)
  starting transfers between devices  35.2 us (30%)
  Pallas kernels  24.4 us (21%)
  other arithmetic  6.94 us (6%)
    pallas_call x2, Pallas kernels, attention(): pl.pallas_call(functools.partial(attention_body, first=first, scale=SCALE...  24.4 us
    ppermute x6, waiting for transfers between devices, shards(): lax.ppermute(unit, axis, [(i, (i + by) % size) for i in range(size)])  15.6 us
    all_to_all x2, waiting for transfers between devices, shards(): lax.all_to_all(both, ('yl', 'z'), split_axis=0, concat_axis=0, tiled=True)  14.8 us
    ppermute x2, waiting for transfers between devices, shards(): unit = lax.ppermute(sent, ('yh', 'c', 'x', 'yl'), to_cross)  11.1 us
    all_to_all x2, starting transfers between devices, shards(): lax.all_to_all(both, ('yl', 'z'), split_axis=0, concat_axis=0, tiled=True)  10.8 us
    ppermute x4, starting transfers between devices, shards(): passed = lax.ppermute(passed, 'x', far)  6.81 us
    ppermute x6, starting transfers between devices, shards(): lax.ppermute(unit, axis, [(i, (i + by) % size) for i in range(size)])  5.97 us
    ppermute x4, starting transfers between devices, shards(): got = lax.ppermute(send, 'x', near)  4.95 us
  transfers between devices with their start and end apart: 20, of which 14 were waited for; matrix products, arithmetic and copies ran while one was open for 3% of the time, Pallas kernels for 10%

profile of v3, /device:TPU:2, one launch (start us, length us, event | category | flops | bytes accessed | tf_op | source)
XLA Modules:
  0.0 117.7 jit_solution(1081776469690067307)
XLA Ops:
  0.7 2.8 %select_bitcast_fusion = (bf16[128,1024]{1,0:T(8,128)(2,1)S(1)}, bf16[128,1024]{1,0:T(8,128)(2,1)}, bf16[1,128,1024]{2,1,0:T(8,128)(2,1)}, bf16[1,128,1024]{2,1,...) fusion(bf16[1,128,8192]{2,1,0:T(8,128)(2,1)} %param.8, s32[]{:T(128)S(6)} %select_n.106, ...), kind=kLoop, calls=%fused_computation.18 | loop fusion | flops 262144 | bytes 3670033 | tf_op jit(solution)/shard_map/jit(_where)/select_n | solution.py:187
  3.5 2.5 %collective-permute-start.6 = (bf16[128,1024]{1,0:T(8,128)(2,1)S(1)}, bf16[128,1024]{1,0:T(8,128)(2,1)S(1)}, u32[]{:S(2)}, u32[]{:S(2)}) collective-permute-start(bf16[128,1024]{1,0:T(8,128)(2,1)S(1)} %get-tuple-element.23), channel_id=1, source_target_pairs={{0,136},{8,128},{16,216},{24,208},{32,168},{40,160},{48,248},{56,2... | collective-permute-start | bytes 786440 | tf_op jit(solution)/shard_map/ppermute | solution.py:191
  7.5 5.5 %collective-permute-done.6.unit_0 = bf16[128,1024]{1,0:T(8,128)(2,1)S(1)} collective-permute-done((bf16[128,1024]{1,0:T(8,128)(2,1)S(1)}, bf16[128,1024]{1,0:T(8,128)(2,1)S(1)}, u32[]{:S(2)}, u32[]{:S(2)}) %collective-permute-start.6) | collective-permute-done | bytes 262176 | tf_op jit(solution)/shard_map/ppermute | solution.py:191
  13.0 1.3 %collective-permute-start.7 = (bf16[128,1024]{1,0:T(8,128)(2,1)S(1)}, bf16[128,1024]{1,0:T(8,128)(2,1)S(1)}, u32[]{:S(2)}, u32[]{:S(2)}) collective-permute-start(bf16[128,1024]{1,0:T(8,128)(2,1)S(1)} %collective-permute-done.6.unit_0), channel_id=1, source_target_pairs={{0,16},{16,32},{32,48},{48,0},{1,17},{17,33},{33,49},{49,1},{2,18}... | collective-permute-start | bytes 786440 | tf_op jit(solution)/shard_map/ppermute | solution.py:195
  15.0 1.9 %collective-permute-start.9 = (bf16[128,1024]{1,0:T(8,128)(2,1)S(1)}, bf16[128,1024]{1,0:T(8,128)(2,1)}, u32[]{:S(2)}, u32[]{:S(2)}) collective-permute-start(bf16[128,1024]{1,0:T(8,128)(2,1)S(1)} %collective-permute-done.6.unit_0), channel_id=1, source_target_pairs={{0,1},{1,2},{2,3},{3,4},{4,5},{5,6},{6,7},{7,0},{8,9},{9,10},{10,1... | collective-permute-start | bytes 786440 | tf_op jit(solution)/shard_map/ppermute | solution.py:195
  17.0 4.3 %collective-permute-done.7.unit_1 = bf16[128,1024]{1,0:T(8,128)(2,1)S(1)} collective-permute-done((bf16[128,1024]{1,0:T(8,128)(2,1)S(1)}, bf16[128,1024]{1,0:T(8,128)(2,1)S(1)}, u32[]{:S(2)}, u32[]{:S(2)}) %collective-permute-start.7) | collective-permute-done | bytes 262176 | tf_op jit(solution)/shard_map/ppermute | solution.py:195
  22.0 5.0 %collective-permute-done.9.unit_3 = bf16[128,1024]{1,0:T(8,128)(2,1)} collective-permute-done((bf16[128,1024]{1,0:T(8,128)(2,1)S(1)}, bf16[128,1024]{1,0:T(8,128)(2,1)}, u32[]{:S(2)}, u32[]{:S(2)}) %collective-permute-start.9) | collective-permute-done | bytes 262176 | tf_op jit(solution)/shard_map/ppermute | solution.py:195
  27.0 12.2 %attention.2 = (bf16[640,2048]{1,0:T(8,128)(2,1)}, bf16[256,1024]{1,0:T(8,128)(2,1)S(1)}, bf16[256,1024]{1,0:T(8,128)(2,1)S(1)}, bf16[256,1024]{1,0:T(8,128)(2,1)S(1)}, bf16[256,1024]{1,0:T(8,128)(2,1)S(1)}) custom-call(s32[17]{0:T(128)S(1)} %stack.87.place, s32[8]{0:T(128)S(1)} %bitcast.47, f32[16]{0:T(128)S(1)} %tanh_bitcast_fusion.factor, ...), custom_call_target="tpu_custom_call" | custom-call | flops 3355443200 | bytes 8388608 | tf_op jit(solution)/shard_map/attention/pallas_call | solution.py:127
  39.3 1.6 %collective-permute-start.10 = (bf16[256,1024]{1,0:T(8,128)(2,1)S(1)}, bf16[256,1024]{1,0:T(8,128)(2,1)S(1)}, u32[]{:S(2)}, u32[]{:S(2)}) collective-permute-start(bf16[256,1024]{1,0:T(8,128)(2,1)S(1)} %get-tuple-element.16), channel_id=1, source_target_pairs={{0,16},{16,0},{32,48},{48,32},{1,17},{17,1},{33,49},{49,33},{2,18}... | collective-permute-start | bytes 1572872 | tf_op jit(solution)/shard_map/ppermute | solution.py:215
  41.9 1.3 %collective-permute-start.1 = (bf16[128,1024]{1,0:T(8,128)(2,1)S(1)}, bf16[128,1024]{1,0:T(8,128)(2,1)S(1)}, u32[]{:S(2)}, u32[]{:S(2)}) collective-permute-start(bf16[128,1024]{1,0:T(8,128)(2,1)S(1)} %copy-done.4), channel_id=1, source_target_pairs={{0,136},{8,128},{16,216},{24,208},{32,168},{40,160},{48,248},{56,2... | collective-permute-start | bytes 786440 | tf_op jit(solution)/shard_map/ppermute | solution.py:191
  43.3 2.2 %collective-permute-start = (bf16[2,128,1024]{2,1,0:T(8,128)(2,1)S(1)}, bf16[2,128,1024]{2,1,0:T(8,128)(2,1)S(1)}, u32[]{:S(2)}, u32[]{:S(2)}) collective-permute-start(bf16[2,128,1024]{2,1,0:T(8,128)(2,1)S(1)} %pad_maximum_fusion), channel_id=1, source_target_pairs={{0,64},{64,0},{1,65},{65,1},{2,66},{66,2},{3,67},{67,3},{4,68},{68... | collective-permute-start | bytes 1572872 | tf_op jit(solution)/shard_map/ppermute | solution.py:192
  45.5 5.6 %collective-permute-done.1.unit_0 = bf16[128,1024]{1,0:T(8,128)(2,1)S(1)} collective-permute-done((bf16[128,1024]{1,0:T(8,128)(2,1)S(1)}, bf16[128,1024]{1,0:T(8,128)(2,1)S(1)}, u32[]{:S(2)}, u32[]{:S(2)}) %collective-permute-start.1) | collective-permute-done | bytes 262176 | tf_op jit(solution)/shard_map/ppermute | solution.py:191
  51.3 1.9 %collective-permute-start.3 = (bf16[128,1024]{1,0:T(8,128)(2,1)S(1)}, bf16[128,1024]{1,0:T(8,128)(2,1)S(1)}, u32[]{:S(2)}, u32[]{:S(2)}) collective-permute-start(bf16[128,1024]{1,0:T(8,128)(2,1)S(1)} %collective-permute-done.1.unit_0), channel_id=1, source_target_pairs={{0,48},{16,0},{32,16},{48,32},{1,49},{17,1},{33,17},{49,33},{2,50}... | collective-permute-start | bytes 786440 | tf_op jit(solution)/shard_map/ppermute | solution.py:195
  54.7 2.2 %collective-permute-start.13 = (bf16[128,1024]{1,0:T(8,128)(2,1)S(1)}, bf16[128,1024]{1,0:T(8,128)(2,1)S(1)}, u32[]{:S(2)}, u32[]{:S(2)}) collective-permute-start(bf16[128,1024]{1,0:T(8,128)(2,1)S(1)} %add_convert_fusion.5), channel_id=1, source_target_pairs={{0,16},{16,0},{32,48},{48,32},{1,17},{17,1},{33,49},{49,33},{2,18}... | collective-permute-start | bytes 786440 | tf_op jit(solution)/shard_map/ppermute | solution.py:217
  56.9 3.4 %collective-permute-done.2.unit_1 = bf16[128,1024]{1,0:T(8,128)(2,1)S(1)} collective-permute-done((bf16[128,1024]{1,0:T(8,128)(2,1)S(1)}, bf16[128,1024]{1,0:T(8,128)(2,1)S(1)}, u32[]{:S(2)}, u32[]{:S(2)}) %collective-permute-start.2) | collective-permute-done | bytes 262176 | tf_op jit(solution)/shard_map/ppermute | solution.py:195
  60.5 2.0 %collective-permute-done.4.unit_3 = bf16[128,1024]{1,0:T(8,128)(2,1)S(1)} collective-permute-done((bf16[128,1024]{1,0:T(8,128)(2,1)S(1)}, bf16[128,1024]{1,0:T(8,128)(2,1)S(1)}, u32[]{:S(2)}, u32[]{:S(2)}) %collective-permute-start.4) | collective-permute-done | bytes 262176 | tf_op jit(solution)/shard_map/ppermute | solution.py:195
  62.5 12.2 %attention.3 = (bf16[640,2048]{1,0:T(8,128)(2,1)}, bf16[256,1024]{1,0:T(8,128)(2,1)}, bf16[256,1024]{1,0:T(8,128)(2,1)S(1)}, bf16[256,1024]{1,0:T(8,128)(2,1)}, bf16[256,1024]{1,0:T(8,128)(2,1)S(1)}) custom-call(s32[17]{0:T(128)S(1)} %stack.87.place, s32[8]{0:T(128)S(1)} %bitcast.48, ...), custom_call_target="tpu_custom_call", output_to_operand_aliasing={{0}: (14, {})} | custom-call | flops 3355443200 | bytes 8388608 | tf_op jit(solution)/shard_map/attention/pallas_call | solution.py:127
  78.1 5.7 %all-to-all-start = ((bf16[16,2,8,1024]{3,2,1,0:T(8,128)(2,1)}), bf16[16,2,8,1024]{3,2,1,0:T(8,128)(2,1)S(1)}, u32[]{:S(2)}, u32[]{:S(2)}) async-start(bf16[16,2,8,1024]{3,2,1,0:T(8,128)(2,1)} %pad_maximum_fusion.2), calls=%async_computation | async-start | bytes 1048576 | tf_op jit(solution)/shard_map/all_to_all | solution.py:224
  83.8 4.0 %collective-permute-done.14 = bf16[256,1024]{1,0:T(8,128)(2,1)S(1)} collective-permute-done((bf16[256,1024]{1,0:T(8,128)(2,1)}, bf16[256,1024]{1,0:T(8,128)(2,1)S(1)}, u32[]{:S(2)}, u32[]{:S(2)}) %collective-permute-start.14) | collective-permute-done | bytes 524320 | tf_op jit(solution)/shard_map/ppermute | solution.py:215
  88.9 2.4 %collective-permute-start.17 = (bf16[128,1024]{1,0:T(8,128)(2,1)S(1)}, bf16[128,1024]{1,0:T(8,128)(2,1)S(1)}, u32[]{:S(2)}, u32[]{:S(2)}) collective-permute-start(bf16[128,1024]{1,0:T(8,128)(2,1)S(1)} %add_convert_fusion.1), channel_id=1, source_target_pairs={{0,16},{16,0},{32,48},{48,32},{1,17},{17,1},{33,49},{49,33},{2,18}... | collective-permute-start | bytes 786440 | tf_op jit(solution)/shard_map/ppermute | solution.py:217
  91.3 3.1 %collective-permute-done.15 = bf16[128,1024]{1,0:T(8,128)(2,1)S(1)} collective-permute-done((bf16[128,1024]{1,0:T(8,128)(2,1)S(1)}, bf16[128,1024]{1,0:T(8,128)(2,1)S(1)}, u32[]{:S(2)}, u32[]{:S(2)}) %collective-permute-start.15) | collective-permute-done | bytes 262176 | tf_op jit(solution)/shard_map/ppermute | solution.py:217
  94.4 1.5 %collective-permute-done.17 = bf16[128,1024]{1,0:T(8,128)(2,1)S(1)} collective-permute-done((bf16[128,1024]{1,0:T(8,128)(2,1)S(1)}, bf16[128,1024]{1,0:T(8,128)(2,1)S(1)}, u32[]{:S(2)}, u32[]{:S(2)}) %collective-permute-start.17) | collective-permute-done | bytes 262176 | tf_op jit(solution)/shard_map/ppermute | solution.py:217
  97.8 5.1 %all-to-all-start.1 = ((bf16[16,2,8,1024]{3,2,1,0:T(8,128)(2,1)}), bf16[16,2,8,1024]{3,2,1,0:T(8,128)(2,1)S(1)}, u32[]{:S(2)}, u32[]{:S(2)}) async-start(bf16[16,2,8,1024]{3,2,1,0:T(8,128)(2,1)} %pad_maximum_fusion.3), calls=%async_computation.1 | async-start | bytes 1048576 | tf_op jit(solution)/shard_map/all_to_all | solution.py:224
  103.1 13.9 %all-to-all-done.1 = bf16[16,2,8,1024]{3,2,1,0:T(8,128)(2,1)S(1)} async-done(((bf16[16,2,8,1024]{3,2,1,0:T(8,128)(2,1)}), bf16[16,2,8,1024]{3,2,1,0:T(8,128)(2,1)S(1)}, u32[]{:S(2)}, u32[]{:S(2)}) %all-to-all-start.1) | async-done | bytes 524320 | tf_op jit(solution)/shard_map/all_to_all | solution.py:224
  (51 shorter events, 13.3 us)
Async XLA Ops:
  0.6 16.3 %copy-start.5 = (s32[640]{0:T(1024)S(1)}, s32[640]{0:T(1024)}, u32[]{:S(2)}) copy-start(s32[640]{0:T(1024)} %param.13) | copy-start | bytes 7684
  0.6 16.4 %copy-start.6 = (f32[1,16]{1,0:T(1,128)S(1)}, f32[1,16]{1,0:T(1,128)}, u32[]{:S(2)}) copy-start(f32[1,16]{1,0:T(1,128)} %param.11) | copy-start | bytes 196
  0.7 26.4 %copy-start = (bf16[1,128,8192]{2,1,0:T(8,128)(2,1)S(1)}, bf16[1,128,8192]{2,1,0:T(8,128)(2,1)}, u32[]{:S(2)}) copy-start(bf16[1,128,8192]{2,1,0:T(8,128)(2,1)} %param.8) | copy-start | bytes 6291460
  0.7 26.4 %copy-start.1 = (s32[1,8]{1,0:T(1,128)S(1)}, s32[1,8]{1,0:T(1,128)}, u32[]{:S(2)}) copy-start(s32[1,8]{1,0:T(1,128)} %param.12) | copy-start | bytes 100
  3.5 9.5 %collective-permute-start.6 = (bf16[128,1024]{1,0:T(8,128)(2,1)S(1)}, bf16[128,1024]{1,0:T(8,128)(2,1)S(1)}, u32[]{:S(2)}, u32[]{:S(2)}) collective-permute-start(bf16[128,1024]{1,0:T(8,128)(2,1)S(1)} %get-tuple-element.23), channel_id=1, source_target_pairs={{0,136},{8,128},{16,216},{24,208},{32,168},{40,160},{48,248},{56,2... | collective-permute-start | bytes 786440 | tf_op jit(solution)/shard_map/ppermute | solution.py:191
  6.8 10.2 %collective-permute-start.5 = (bf16[2,128,1024]{2,1,0:T(8,128)(2,1)}, bf16[2,128,1024]{2,1,0:T(8,128)(2,1)S(1)}, u32[]{:S(2)}, u32[]{:S(2)}) collective-permute-start(bf16[2,128,1024]{2,1,0:T(8,128)(2,1)} %pad_maximum_fusion.1), channel_id=1, source_target_pairs={{0,64},{64,0},{1,65},{65,1},{2,66},{66,2},{3,67},{67,3},{4,68},{68... | collective-permute-start | bytes 1572872 | tf_op jit(solution)/shard_map/ppermute | solution.py:192
  13.0 8.4 %collective-permute-start.7 = (bf16[128,1024]{1,0:T(8,128)(2,1)S(1)}, bf16[128,1024]{1,0:T(8,128)(2,1)S(1)}, u32[]{:S(2)}, u32[]{:S(2)}) collective-permute-start(bf16[128,1024]{1,0:T(8,128)(2,1)S(1)} %collective-permute-done.6.unit_0), channel_id=1, source_target_pairs={{0,16},{16,32},{32,48},{48,0},{1,17},{17,33},{33,49},{49,1},{2,18}... | collective-permute-start | bytes 786440 | tf_op jit(solution)/shard_map/ppermute | solution.py:195
  14.3 7.7 %collective-permute-start.8 = (bf16[128,1024]{1,0:T(8,128)(2,1)S(1)}, bf16[128,1024]{1,0:T(8,128)(2,1)S(1)}, u32[]{:S(2)}, u32[]{:S(2)}) collective-permute-start(bf16[128,1024]{1,0:T(8,128)(2,1)S(1)} %collective-permute-done.6.unit_0), channel_id=1, source_target_pairs={{0,48},{16,0},{32,16},{48,32},{1,49},{17,1},{33,17},{49,33},{2,50}... | collective-permute-start | bytes 786440 | tf_op jit(solution)/shard_map/ppermute | solution.py:195
  15.0 12.0 %collective-permute-start.9 = (bf16[128,1024]{1,0:T(8,128)(2,1)S(1)}, bf16[128,1024]{1,0:T(8,128)(2,1)}, u32[]{:S(2)}, u32[]{:S(2)}) collective-permute-start(bf16[128,1024]{1,0:T(8,128)(2,1)S(1)} %collective-permute-done.6.unit_0), channel_id=1, source_target_pairs={{0,1},{1,2},{2,3},{3,4},{4,5},{5,6},{6,7},{7,0},{8,9},{9,10},{10,1... | collective-permute-start | bytes 786440 | tf_op jit(solution)/shard_map/ppermute | solution.py:195
  39.3 13.9 %collective-permute-start.10 = (bf16[256,1024]{1,0:T(8,128)(2,1)S(1)}, bf16[256,1024]{1,0:T(8,128)(2,1)S(1)}, u32[]{:S(2)}, u32[]{:S(2)}) collective-permute-start(bf16[256,1024]{1,0:T(8,128)(2,1)S(1)} %get-tuple-element.16), channel_id=1, source_target_pairs={{0,16},{16,0},{32,48},{48,32},{1,17},{17,1},{33,49},{49,33},{2,18}... | collective-permute-start | bytes 1572872 | tf_op jit(solution)/shard_map/ppermute | solution.py:215
  40.8 12.5 %collective-permute-start.12 = (bf16[256,1024]{1,0:T(8,128)(2,1)S(1)}, bf16[256,1024]{1,0:T(8,128)(2,1)S(1)}, u32[]{:S(2)}, u32[]{:S(2)}) collective-permute-start(bf16[256,1024]{1,0:T(8,128)(2,1)S(1)} %get-tuple-element.18), channel_id=1, source_target_pairs={{0,48},{16,32},{32,16},{48,0},{1,49},{17,33},{33,17},{49,1},{2,50}... | collective-permute-start | bytes 1572872 | tf_op jit(solution)/shard_map/ppermute | solution.py:215
  41.9 9.2 %collective-permute-start.1 = (bf16[128,1024]{1,0:T(8,128)(2,1)S(1)}, bf16[128,1024]{1,0:T(8,128)(2,1)S(1)}, u32[]{:S(2)}, u32[]{:S(2)}) collective-permute-start(bf16[128,1024]{1,0:T(8,128)(2,1)S(1)} %copy-done.4), channel_id=1, source_target_pairs={{0,136},{8,128},{16,216},{24,208},{32,168},{40,160},{48,248},{56,2... | collective-permute-start | bytes 786440 | tf_op jit(solution)/shard_map/ppermute | solution.py:191
  43.3 11.3 %collective-permute-start = (bf16[2,128,1024]{2,1,0:T(8,128)(2,1)S(1)}, bf16[2,128,1024]{2,1,0:T(8,128)(2,1)S(1)}, u32[]{:S(2)}, u32[]{:S(2)}) collective-permute-start(bf16[2,128,1024]{2,1,0:T(8,128)(2,1)S(1)} %pad_maximum_fusion), channel_id=1, source_target_pairs={{0,64},{64,0},{1,65},{65,1},{2,66},{66,2},{3,67},{67,3},{4,68},{68... | collective-permute-start | bytes 1572872 | tf_op jit(solution)/shard_map/ppermute | solution.py:192
  51.1 9.2 %collective-permute-start.2 = (bf16[128,1024]{1,0:T(8,128)(2,1)S(1)}, bf16[128,1024]{1,0:T(8,128)(2,1)S(1)}, u32[]{:S(2)}, u32[]{:S(2)}) collective-permute-start(bf16[128,1024]{1,0:T(8,128)(2,1)S(1)} %collective-permute-done.1.unit_0), channel_id=1, source_target_pairs={{0,16},{16,32},{32,48},{48,0},{1,17},{17,33},{33,49},{49,1},{2,18}... | collective-permute-start | bytes 786440 | tf_op jit(solution)/shard_map/ppermute | solution.py:195
  51.3 9.2 %collective-permute-start.3 = (bf16[128,1024]{1,0:T(8,128)(2,1)S(1)}, bf16[128,1024]{1,0:T(8,128)(2,1)S(1)}, u32[]{:S(2)}, u32[]{:S(2)}) collective-permute-start(bf16[128,1024]{1,0:T(8,128)(2,1)S(1)} %collective-permute-done.1.unit_0), channel_id=1, source_target_pairs={{0,48},{16,0},{32,16},{48,32},{1,49},{17,1},{33,17},{49,33},{2,50}... | collective-permute-start | bytes 786440 | tf_op jit(solution)/shard_map/ppermute | solution.py:195
  53.2 9.3 %collective-permute-start.4 = (bf16[128,1024]{1,0:T(8,128)(2,1)S(1)}, bf16[128,1024]{1,0:T(8,128)(2,1)S(1)}, u32[]{:S(2)}, u32[]{:S(2)}) collective-permute-start(bf16[128,1024]{1,0:T(8,128)(2,1)S(1)} %collective-permute-done.1.unit_0), channel_id=1, source_target_pairs={{0,1},{1,2},{2,3},{3,4},{4,5},{5,6},{6,7},{7,0},{8,9},{9,10},{10,1... | collective-permute-start | bytes 786440 | tf_op jit(solution)/shard_map/ppermute | solution.py:195
  53.3 23.6 %collective-permute-start.11 = (bf16[128,1024]{1,0:T(8,128)(2,1)S(1)}, bf16[128,1024]{1,0:T(8,128)(2,1)S(1)}, u32[]{:S(2)}, u32[]{:S(2)}) collective-permute-start(bf16[128,1024]{1,0:T(8,128)(2,1)S(1)} %add_convert_fusion.7), channel_id=1, source_target_pairs={{0,48},{16,32},{32,16},{48,0},{1,49},{17,33},{33,17},{49,1},{2,50}... | collective-permute-start | bytes 786440 | tf_op jit(solution)/shard_map/ppermute | solution.py:217
  54.7 22.4 %collective-permute-start.13 = (bf16[128,1024]{1,0:T(8,128)(2,1)S(1)}, bf16[128,1024]{1,0:T(8,128)(2,1)S(1)}, u32[]{:S(2)}, u32[]{:S(2)}) collective-permute-start(bf16[128,1024]{1,0:T(8,128)(2,1)S(1)} %add_convert_fusion.5), channel_id=1, source_target_pairs={{0,16},{16,0},{32,48},{48,32},{1,17},{17,1},{33,49},{49,33},{2,18}... | collective-permute-start | bytes 786440 | tf_op jit(solution)/shard_map/ppermute | solution.py:217
  74.7 13.1 %collective-permute-start.14 = (bf16[256,1024]{1,0:T(8,128)(2,1)}, bf16[256,1024]{1,0:T(8,128)(2,1)S(1)}, u32[]{:S(2)}, u32[]{:S(2)}) collective-permute-start(bf16[256,1024]{1,0:T(8,128)(2,1)} %get-tuple-element.20), channel_id=1, source_target_pairs={{0,16},{16,0},{32,48},{48,32},{1,17},{17,1},{33,49},{49,33},{2,18}... | collective-permute-start | bytes 1572872 | tf_op jit(solution)/shard_map/ppermute | solution.py:215
  75.8 13.0 %collective-permute-start.16 = (bf16[256,1024]{1,0:T(8,128)(2,1)}, bf16[256,1024]{1,0:T(8,128)(2,1)S(1)}, u32[]{:S(2)}, u32[]{:S(2)}) collective-permute-start(bf16[256,1024]{1,0:T(8,128)(2,1)} %get-tuple-element.22), channel_id=1, source_target_pairs={{0,48},{16,32},{32,16},{48,0},{1,49},{17,33},{33,17},{49,1},{2,50}... | collective-permute-start | bytes 1572872 | tf_op jit(solution)/shard_map/ppermute | solution.py:215
  78.1 19.7 %all-to-all-start = ((bf16[16,2,8,1024]{3,2,1,0:T(8,128)(2,1)}), bf16[16,2,8,1024]{3,2,1,0:T(8,128)(2,1)S(1)}, u32[]{:S(2)}, u32[]{:S(2)}) async-start(bf16[16,2,8,1024]{3,2,1,0:T(8,128)(2,1)} %pad_maximum_fusion.2), calls=%async_computation | async-start | bytes 1048576 | tf_op jit(solution)/shard_map/all_to_all | solution.py:224
  87.8 6.5 %collective-permute-start.15 = (bf16[128,1024]{1,0:T(8,128)(2,1)S(1)}, bf16[128,1024]{1,0:T(8,128)(2,1)S(1)}, u32[]{:S(2)}, u32[]{:S(2)}) collective-permute-start(bf16[128,1024]{1,0:T(8,128)(2,1)S(1)} %add_convert_fusion.3), channel_id=1, source_target_pairs={{0,48},{16,32},{32,16},{48,0},{1,49},{17,33},{33,17},{49,1},{2,50}... | collective-permute-start | bytes 786440 | tf_op jit(solution)/shard_map/ppermute | solution.py:217
  88.9 7.1 %collective-permute-start.17 = (bf16[128,1024]{1,0:T(8,128)(2,1)S(1)}, bf16[128,1024]{1,0:T(8,128)(2,1)S(1)}, u32[]{:S(2)}, u32[]{:S(2)}) collective-permute-start(bf16[128,1024]{1,0:T(8,128)(2,1)S(1)} %add_convert_fusion.1), channel_id=1, source_target_pairs={{0,16},{16,0},{32,48},{48,32},{1,17},{17,1},{33,49},{49,33},{2,18}... | collective-permute-start | bytes 786440 | tf_op jit(solution)/shard_map/ppermute | solution.py:217
  97.8 19.1 %all-to-all-start.1 = ((bf16[16,2,8,1024]{3,2,1,0:T(8,128)(2,1)}), bf16[16,2,8,1024]{3,2,1,0:T(8,128)(2,1)S(1)}, u32[]{:S(2)}, u32[]{:S(2)}) async-start(bf16[16,2,8,1024]{3,2,1,0:T(8,128)(2,1)} %pad_maximum_fusion.3), calls=%async_computation.1 | async-start | bytes 1048576 | tf_op jit(solution)/shard_map/all_to_all | solution.py:224
  (3 other events, 47.4 us)

commit v4 on v3

--- a/solution.py
+++ b/solution.py
@@ -103,6 +103,11 @@
     own_of = lambda h, place: (0, place[0] // step + first // step + h)
     part = lambda rows, at=0: pl.BlockSpec((rows, width), lambda h, place: (0, at // step + h))
     paired = lambda which: pl.BlockSpec((1, 128, width), lambda h, place: (which, 0, offset // step + h))
+    if len(units) == 2:
+        units = [u for u in units for _ in range(2)]
+        unit_specs = [paired(0), paired(1)] * 2
+    else:
+        unit_specs = [part(128, offset)] * 4
     grads = jax.ShapeDtypeStruct((256, count * HEAD), jnp.bfloat16)
     grid_spec = pltpu.PrefetchScalarGridSpec(
         num_scalar_prefetch=1,
@@ -118,7 +123,7 @@
             paired(0),
             paired(1),
         ]
-        + [part(128, offset)] * 4
+        + unit_specs
         + [pl.BlockSpec(memory_space=pl.ANY)] * len(buffer),
         out_specs=[pl.BlockSpec((tokens, width), head_of)] + [part(256)] * 4,
         scratch_shapes=[pltpu.VMEM((1024, width), jnp.bfloat16)],
@@ -129,7 +134,7 @@
         grid_spec=grid_spec,
         out_shape=[jax.ShapeDtypeStruct(query.shape, jnp.bfloat16)] + [grads] * 4,
         input_output_aliases={14: 0} if buffer else {},
-        compiler_params=pltpu.CompilerParams(dimension_semantics=("arbitrary",), vmem_limit_bytes=48 * 2**20),
+        compiler_params=pltpu.CompilerParams(dimension_semantics=("arbitrary",), vmem_limit_bytes=51 * 2**20),
         cost_estimate=pl.CostEstimate(
             flops=5 * count * matmul, transcendentals=count * tokens * 512, bytes_accessed=count * 2**20
         ),
@@ -168,9 +173,10 @@
     own = yh * 2 + c
     pair_owner = yh * 2 + 1 - c
     place = [own * heads, row_block(own), 512 + row_block(own), row_block(pair_owner), 512 + row_block(pair_owner)]
-    place += [unit_at(colour(x + dx, z + dz, c)) for dx, dz in ((0, 0), (3, 0), (1, 0), (0, 7))]
-    place += [(x ^ flip) * 2 + half for flip in (2, 1, 3, 0) for half in (0, 1)]
-    place = jnp.stack(place).astype(jnp.int32)
+    quarters = [unit_at(colour(x + dx, z + dz, c)) for dx, dz in ((0, 0), (3, 0), (1, 0), (0, 7))]
+    halves = [unit_at(2 * kind + (x ^ c ^ away) % 2) for away in (0, 1) for kind in (0, 1)]
+    images = [(x ^ flip) * 2 + half for flip in (2, 1, 3, 0) for half in (0, 1)]
+    places = [jnp.stack(place + units + images).astype(jnp.int32) for units in (quarters, halves)]
     factor = jnp.tanh(gate_value[0])
     seen = image_seen[None]
 
@@ -182,27 +188,30 @@
 
     gathered = []
     first = 0
-    for counts in GATHERS:
+    shift = lambda array, axis, size, by: lax.ppermute(array, axis, [(i, (i + by) % size) for i in range(size)])
+    for n, counts in enumerate(GATHERS):
         at, width = first * HEAD, sum(counts) * HEAD
-        sent = jnp.where(
-            wants_values, columns(values, there * local + at, width), columns(keys, there * local + at, width)
-        )
-        pair = jnp.stack([columns(a, pair_owner * local + at, width) for a in (keys, values)])
+        sent = [columns(a, there * local + at, width) for a in (keys, values)]
+        sent = jnp.stack(sent) if n else jnp.where(wants_values, sent[1], sent[0])
+        if n == 0:
+            keys_too, values_too, sent = lax.optimization_barrier((keys, values, sent))
+        pair = jnp.stack([columns(a, pair_owner * local + at, width) for a in (keys_too, values_too)])
         unit = lax.ppermute(sent, ("yh", "c", "x", "yl"), to_cross)
         pair = lax.ppermute(pair, "c", [(0, 1), (1, 0)])
-        units = [unit]
-        for axis, size, by in (("x", 4, 1), ("x", 4, 3), ("z", 8, 1)):
-            units.append(lax.ppermute(unit, axis, [(i, (i + by) % size) for i in range(size)]))
+        if n:
+            units = [unit, lax.ppermute(unit, "x", flip_pairs)]
+        else:
+            units = [unit] + [shift(unit, *move) for move in (("x", 4, 1), ("x", 4, 3), ("z", 8, 1))]
         offset = 0
         for count in counts:
-            gathered.append((pair, units, first, count, offset))
+            gathered.append((places[n > 0], pair, units, first, count, offset))
             first += count
             offset += count
 
     buffer = ()
     ready, parts = [], []
     f32 = jnp.float32
-    for pair, units, first, count, offset in gathered:
+    for place, pair, units, first, count, offset in gathered:
         whole, key_send, key_keep, value_send, value_keep = attention(
             place, image_order[0], factor, seen, query, grad_in, keys, values, pair, units,
             buffer, first, count, offset,

time: 119 us -> 123 us (1.034)
  the two profiles are of different devices: /device:TPU:2 before, /device:TPU:16 now
where the time goes in v4:
time: 123 us; the launch traced here: 122 us
  waiting for transfers between devices  49.1 us (40%)
  starting transfers between devices  31.5 us (26%)
  Pallas kernels  24.7 us (20%)
  other arithmetic  14 us (11%)
  local copies, waits for them, and re-layouts  2.31 us (2%)
    pallas_call x2, Pallas kernels, attention(): pl.pallas_call(functools.partial(attention_body, first=first, scale=SCALE...  24.7 us
    all_to_all x2, starting transfers between devices, shards(): lax.all_to_all(both, ('yl', 'z'), split_axis=0, concat_axis=0, tiled=True)  15.7 us
    all_to_all x2, waiting for transfers between devices, shards(): lax.all_to_all(both, ('yl', 'z'), split_axis=0, concat_axis=0, tiled=True)  11.4 us
    ppermute x4, waiting for transfers between devices, shards(): got = lax.ppermute(send, 'x', near)  10.8 us
    ppermute x3, waiting for transfers between devices, shards(): lax.ppermute(array, axis, [(i, (i + by) % size) for i in range(size)])  8.86 us
    ppermute x1, waiting for transfers between devices, shards(): units = [unit, lax.ppermute(unit, 'x', flip_pairs)]  6.94 us
    ppermute x2, waiting for transfers between devices, shards(): unit = lax.ppermute(sent, ('yh', 'c', 'x', 'yl'), to_cross)  6.13 us
    another operation x6, other arithmetic, shards(): jnp.stack([m.reshape(16, 8, count * HEAD) for m in mine], axis=1)  6.01 us
  transfers between devices with their start and end apart: 18, of which 9 were waited for; matrix products, arithmetic and copies ran while one was open for 11% of the time, Pallas kernels for 20%

profile of v4, /device:TPU:16, one launch (start us, length us, event | category | flops | bytes accessed | tf_op | source)
XLA Modules:
  0.0 122.5 jit_solution(1584808608169589847)
XLA Ops:
  0.7 1.3 %constant_dynamic-slice_fusion.1 = (bf16[1,128,1024]{2,1,0:T(8,128)(2,1)S(1)}, bf16[128,1024]{1,0:T(8,128)(2,1)S(1)}, bf16[1,128,1024]{2,1,0:T(8,128)(2,1)S(1)}) fusion(bf16[1,128,8192]{2,1,0:T(8,128)(2,1)} %param.8, s32[]{:T(128)S(6)} %select_n.137, s32[]{:T(128)S(6)} %select_n.133, bf16[1,128,8192]{2,1,0:T(8,128)(2,1)} %param.9, pred[]{:T(512)S(6)} %eq.21), kind=kLoop, calls=%fused_computation.30 | loop fusion | flops 131072 | bytes 1835017 | tf_op jit(solution)/shard_map/dynamic_slice | solution.py:161
  2.5 1.3 %dynamic-slice_bitcast_fusion = (bf16[1,128,1024]{2,1,0:T(8,128)(2,1)S(1)}, bf16[1,128,1024]{2,1,0:T(8,128)(2,1)S(1)}, bf16[1,128,1024]{2,1,0:T(8,128)(2,1)S(1)}, bf16[1,128,1024]{2,1,0:T(8,128)(2,1)S(1)}) fusion(bf16[128,8192]{1,0:T(8,128)(2,1)} %bitcast.60, s32[]{:T(128)S(6)} %select_n.149, s32[]{:T(128)S(6)} %select_n.136, bf16[128,8192]{1,0:T(8,128)(2,1)} %bitcast.57), kind=kLoop, calls=%fused_computation.19 | loop fusion | bytes 2097160 | tf_op jit(solution)/shard_map/stack | solution.py:198
  4.0 6.1 %collective-permute-done.4.unit_0 = bf16[128,1024]{1,0:T(8,128)(2,1)S(1)} collective-permute-done((bf16[128,1024]{1,0:T(8,128)(2,1)S(1)}, bf16[128,1024]{1,0:T(8,128)(2,1)S(1)}, u32[]{:S(2)}, u32[]{:S(2)}) %collective-permute-start.4) | collective-permute-done | bytes 262176 | tf_op jit(solution)/shard_map/ppermute | solution.py:199
  10.1 2.0 %collective-permute-start.5 = (bf16[128,1024]{1,0:T(8,128)(2,1)S(1)}, bf16[128,1024]{1,0:T(8,128)(2,1)S(1)}, u32[]{:S(2)}, u32[]{:S(2)}) collective-permute-start(bf16[128,1024]{1,0:T(8,128)(2,1)S(1)} %collective-permute-done.4.unit_0), channel_id=1, source_target_pairs={{0,16},{16,32},{32,48},{48,0},{1,17},{17,33},{33,49},{49,1},{2,18}... | collective-permute-start | bytes 786440 | tf_op jit(solution)/shard_map/ppermute | solution.py:191
  12.2 1.3 %collective-permute-start.6 = (bf16[128,1024]{1,0:T(8,128)(2,1)S(1)}, bf16[128,1024]{1,0:T(8,128)(2,1)S(1)}, u32[]{:S(2)}, u32[]{:S(2)}) collective-permute-start(bf16[128,1024]{1,0:T(8,128)(2,1)S(1)} %collective-permute-done.4.unit_0), channel_id=1, source_target_pairs={{0,48},{16,0},{32,16},{48,32},{1,49},{17,1},{33,17},{49,33},{2,50}... | collective-permute-start | bytes 786440 | tf_op jit(solution)/shard_map/ppermute | solution.py:191
  13.4 1.9 %collective-permute-start.7 = (bf16[128,1024]{1,0:T(8,128)(2,1)S(1)}, bf16[128,1024]{1,0:T(8,128)(2,1)S(1)}, u32[]{:S(2)}, u32[]{:S(2)}) collective-permute-start(bf16[128,1024]{1,0:T(8,128)(2,1)S(1)} %collective-permute-done.4.unit_0), channel_id=1, source_target_pairs={{0,1},{1,2},{2,3},{3,4},{4,5},{5,6},{6,7},{7,0},{8,9},{9,10},{10,1... | collective-permute-start | bytes 786440 | tf_op jit(solution)/shard_map/ppermute | solution.py:191
  16.7 3.3 %collective-permute-done.5.unit_1 = bf16[128,1024]{1,0:T(8,128)(2,1)S(1)} collective-permute-done((bf16[128,1024]{1,0:T(8,128)(2,1)S(1)}, bf16[128,1024]{1,0:T(8,128)(2,1)S(1)}, u32[]{:S(2)}, u32[]{:S(2)}) %collective-permute-start.5) | collective-permute-done | bytes 262176 | tf_op jit(solution)/shard_map/ppermute | solution.py:191
  20.2 5.4 %collective-permute-done.7.unit_3 = bf16[128,1024]{1,0:T(8,128)(2,1)S(1)} collective-permute-done((bf16[128,1024]{1,0:T(8,128)(2,1)S(1)}, bf16[128,1024]{1,0:T(8,128)(2,1)S(1)}, u32[]{:S(2)}, u32[]{:S(2)}) %collective-permute-start.7) | collective-permute-done | bytes 262176 | tf_op jit(solution)/shard_map/ppermute | solution.py:191
  25.6 12.4 %attention.2 = (bf16[640,2048]{1,0:T(8,128)(2,1)}, bf16[256,1024]{1,0:T(8,128)(2,1)S(1)}, bf16[256,1024]{1,0:T(8,128)(2,1)S(1)}, bf16[256,1024]{1,0:T(8,128)(2,1)S(1)}, bf16[256,1024]{1,0:T(8,128)(2,1)}) custom-call(s32[17]{0:T(128)S(1)} %stack.137.place, s32[8]{0:T(128)S(1)} %bitcast.55, f32[16]{0:T(128)S(1)} %tanh_bitcast_fusion.factor, ...), custom_call_target="tpu_custom_call" | custom-call | flops 3355443200 | bytes 8388608 | tf_op jit(solution)/shard_map/attention/pallas_call | solution.py:132
  38.5 1.5 %collective-permute-start.10 = (bf16[256,1024]{1,0:T(8,128)(2,1)S(1)}, bf16[256,1024]{1,0:T(8,128)(2,1)}, u32[]{:S(2)}, u32[]{:S(2)}) collective-permute-start(bf16[256,1024]{1,0:T(8,128)(2,1)S(1)} %get-tuple-element.24), channel_id=1, source_target_pairs={{0,48},{16,32},{32,16},{48,0},{1,49},{17,33},{33,17},{49,1},{2,50}... | collective-permute-start | bytes 1572872 | tf_op jit(solution)/shard_map/ppermute | solution.py:224
  40.9 1.1 collective-permute-start.2
  42.2 10.8 %collective-permute-done.8 = bf16[256,1024]{1,0:T(8,128)(2,1)} collective-permute-done((bf16[256,1024]{1,0:T(8,128)(2,1)S(1)}, bf16[256,1024]{1,0:T(8,128)(2,1)}, u32[]{:S(2)}, u32[]{:S(2)}) %collective-permute-start.8) | collective-permute-done | bytes 524320 | tf_op jit(solution)/shard_map/ppermute | solution.py:224
  54.0 2.0 %collective-permute-start.9 = (bf16[128,1024]{1,0:T(8,128)(2,1)S(1)}, bf16[128,1024]{1,0:T(8,128)(2,1)S(1)}, u32[]{:S(2)}, u32[]{:S(2)}) collective-permute-start(bf16[128,1024]{1,0:T(8,128)(2,1)S(1)} %add_convert_fusion.7), channel_id=1, source_target_pairs={{0,48},{16,32},{32,16},{48,0},{1,49},{17,33},{33,17},{49,1},{2,50}... | collective-permute-start | bytes 786440 | tf_op jit(solution)/shard_map/ppermute | solution.py:226
  57.1 6.9 %collective-permute-done.2.unit_2.unit_3 = bf16[2,128,1024]{2,1,0:T(8,128)(2,1)S(1)} collective-permute-done((bf16[2,128,1024]{2,1,0:T(8,128)(2,1)}, bf16[2,128,1024]{2,1,0:T(8,128)(2,1)S(1)}, u32[]{:S(2)}, u32[]{:S(2)}) %collective-permute-start.2) | collective-permute-done | bytes 524320 | tf_op jit(solution)/shard_map/ppermute | solution.py:202
  64.9 12.4 %attention.3 = (bf16[640,2048]{1,0:T(8,128)(2,1)}, bf16[256,1024]{1,0:T(8,128)(2,1)S(1)}, bf16[256,1024]{1,0:T(8,128)(2,1)S(1)}, bf16[256,1024]{1,0:T(8,128)(2,1)S(1)}, bf16[256,1024]{1,0:T(8,128)(2,1)S(1)}) custom-call(s32[17]{0:T(128)S(1)} %stack.128.place, s32[8]{0:T(128)S(1)} %bitcast.56, ...), custom_call_target="tpu_custom_call", output_to_operand_aliasing={{0}: (14, {})} | custom-call | flops 3355443200 | bytes 8388608 | tf_op jit(solution)/shard_map/attention/pallas_call | solution.py:132
  77.7 1.5 %collective-permute-start.14 = (bf16[256,1024]{1,0:T(8,128)(2,1)S(1)}, bf16[256,1024]{1,0:T(8,128)(2,1)}, u32[]{:S(2)}, u32[]{:S(2)}) collective-permute-start(bf16[256,1024]{1,0:T(8,128)(2,1)S(1)} %get-tuple-element.28), channel_id=1, source_target_pairs={{0,48},{16,32},{32,16},{48,0},{1,49},{17,33},{33,17},{49,1},{2,50}... | collective-permute-start | bytes 1572872 | tf_op jit(solution)/shard_map/ppermute | solution.py:224
  79.3 1.1 fusion
  80.4 1.1 fusion.1
  82.3 7.6 %all-to-all-start = ((bf16[16,2,8,1024]{3,2,1,0:T(8,128)(2,1)}), bf16[16,2,8,1024]{3,2,1,0:T(8,128)(2,1)S(1)}, u32[]{:S(2)}, u32[]{:S(2)}) async-start(bf16[16,2,8,1024]{3,2,1,0:T(8,128)(2,1)} %pad_maximum_fusion.3), calls=%async_computation | async-start | bytes 1048576 | tf_op jit(solution)/shard_map/all_to_all | solution.py:233
  91.0 1.8 %collective-permute-start.13 = (bf16[128,1024]{1,0:T(8,128)(2,1)S(1)}, bf16[128,1024]{1,0:T(8,128)(2,1)S(1)}, u32[]{:S(2)}, u32[]{:S(2)}) collective-permute-start(bf16[128,1024]{1,0:T(8,128)(2,1)S(1)} %add_convert_fusion.3), channel_id=1, source_target_pairs={{0,48},{16,32},{32,16},{48,0},{1,49},{17,33},{33,17},{49,1},{2,50}... | collective-permute-start | bytes 786440 | tf_op jit(solution)/shard_map/ppermute | solution.py:226
  94.2 4.4 %collective-permute-done.13 = bf16[128,1024]{1,0:T(8,128)(2,1)S(1)} collective-permute-done((bf16[128,1024]{1,0:T(8,128)(2,1)S(1)}, bf16[128,1024]{1,0:T(8,128)(2,1)S(1)}, u32[]{:S(2)}, u32[]{:S(2)}) %collective-permute-start.13) | collective-permute-done | bytes 262176 | tf_op jit(solution)/shard_map/ppermute | solution.py:226
  98.7 1.1 fusion.2
  102.2 8.1 %all-to-all-start.1 = ((bf16[16,2,8,1024]{3,2,1,0:T(8,128)(2,1)}), bf16[16,2,8,1024]{3,2,1,0:T(8,128)(2,1)S(1)}, u32[]{:S(2)}, u32[]{:S(2)}) async-start(bf16[16,2,8,1024]{3,2,1,0:T(8,128)(2,1)} %pad_maximum_fusion.4), calls=%async_computation.1 | async-start | bytes 1048576 | tf_op jit(solution)/shard_map/all_to_all | solution.py:233
  110.4 11.4 %all-to-all-done.1 = bf16[16,2,8,1024]{3,2,1,0:T(8,128)(2,1)S(1)} async-done(((bf16[16,2,8,1024]{3,2,1,0:T(8,128)(2,1)}), bf16[16,2,8,1024]{3,2,1,0:T(8,128)(2,1)S(1)}, u32[]{:S(2)}, u32[]{:S(2)}) %all-to-all-start.1) | async-done | bytes 524320 | tf_op jit(solution)/shard_map/all_to_all | solution.py:233
  (50 shorter events, 13.8 us)
Async XLA Ops:
  2.0 8.1 %collective-permute-start.4 = (bf16[128,1024]{1,0:T(8,128)(2,1)S(1)}, bf16[128,1024]{1,0:T(8,128)(2,1)S(1)}, u32[]{:S(2)}, u32[]{:S(2)}) collective-permute-start(bf16[128,1024]{1,0:T(8,128)(2,1)S(1)} %get-tuple-element.18), channel_id=1, source_target_pairs={{0,136},{8,128},{16,216},{24,208},{32,168},{40,160},{48,248},{56,2... | collective-permute-start | bytes 786440 | tf_op jit(solution)/shard_map/ppermute | solution.py:199
  2.5 14.1 %copy-start.4 = (s32[640]{0:T(1024)S(1)}, s32[640]{0:T(1024)}, u32[]{:S(2)}) copy-start(s32[640]{0:T(1024)} %param.13) | copy-start | bytes 7684
  2.5 14.2 %copy-start.6 = (f32[1,16]{1,0:T(1,128)S(1)}, f32[1,16]{1,0:T(1,128)}, u32[]{:S(2)}) copy-start(f32[1,16]{1,0:T(1,128)} %param.11) | copy-start | bytes 196
  2.5 23.1 %copy-start = (s32[1,8]{1,0:T(1,128)S(1)}, s32[1,8]{1,0:T(1,128)}, u32[]{:S(2)}) copy-start(s32[1,8]{1,0:T(1,128)} %param.12) | copy-start | bytes 100
  3.9 12.8 %collective-permute-start.3 = (bf16[2,128,1024]{2,1,0:T(8,128)(2,1)S(1)}, bf16[2,128,1024]{2,1,0:T(8,128)(2,1)S(1)}, u32[]{:S(2)}, u32[]{:S(2)}) collective-permute-start(bf16[2,128,1024]{2,1,0:T(8,128)(2,1)S(1)} %pad_maximum_fusion.2), channel_id=1, source_target_pairs={{0,64},{64,0},{1,65},{65,1},{2,66},{66,2},{3,67},{67,3},{4,68},{68... | collective-permute-start | bytes 1572872 | tf_op jit(solution)/shard_map/ppermute | solution.py:200
  10.1 9.9 %collective-permute-start.5 = (bf16[128,1024]{1,0:T(8,128)(2,1)S(1)}, bf16[128,1024]{1,0:T(8,128)(2,1)S(1)}, u32[]{:S(2)}, u32[]{:S(2)}) collective-permute-start(bf16[128,1024]{1,0:T(8,128)(2,1)S(1)} %collective-permute-done.4.unit_0), channel_id=1, source_target_pairs={{0,16},{16,32},{32,48},{48,0},{1,17},{17,33},{33,49},{49,1},{2,18}... | collective-permute-start | bytes 786440 | tf_op jit(solution)/shard_map/ppermute | solution.py:191
  12.2 8.0 %collective-permute-start.6 = (bf16[128,1024]{1,0:T(8,128)(2,1)S(1)}, bf16[128,1024]{1,0:T(8,128)(2,1)S(1)}, u32[]{:S(2)}, u32[]{:S(2)}) collective-permute-start(bf16[128,1024]{1,0:T(8,128)(2,1)S(1)} %collective-permute-done.4.unit_0), channel_id=1, source_target_pairs={{0,48},{16,0},{32,16},{48,32},{1,49},{17,1},{33,17},{49,33},{2,50}... | collective-permute-start | bytes 786440 | tf_op jit(solution)/shard_map/ppermute | solution.py:191
  13.4 12.2 %collective-permute-start.7 = (bf16[128,1024]{1,0:T(8,128)(2,1)S(1)}, bf16[128,1024]{1,0:T(8,128)(2,1)S(1)}, u32[]{:S(2)}, u32[]{:S(2)}) collective-permute-start(bf16[128,1024]{1,0:T(8,128)(2,1)S(1)} %collective-permute-done.4.unit_0), channel_id=1, source_target_pairs={{0,1},{1,2},{2,3},{3,4},{4,5},{5,6},{6,7},{7,0},{8,9},{9,10},{10,1... | collective-permute-start | bytes 786440 | tf_op jit(solution)/shard_map/ppermute | solution.py:191
  16.2 24.7 %collective-permute-start.1 = (bf16[2,128,1024]{2,1,0:T(8,128)(2,1)}, bf16[2,128,1024]{2,1,0:T(8,128)(2,1)}, u32[]{:S(2)}, u32[]{:S(2)}) collective-permute-start(bf16[2,128,1024]{2,1,0:T(8,128)(2,1)} %pad_maximum_fusion.1), channel_id=1, source_target_pairs={{0,136},{8,128},{16,216},{24,208},{32,168},{40,160},{48,248},{56,2... | collective-permute-start | bytes 1572872 | tf_op jit(solution)/shard_map/ppermute | solution.py:199
  16.7 8.9 %copy-start.5 = (bf16[2,128,1024]{2,1,0:T(8,128)(2,1)}, bf16[2,128,1024]{2,1,0:T(8,128)(2,1)S(1)}, u32[]{:S(2)}) copy-start(bf16[2,128,1024]{2,1,0:T(8,128)(2,1)S(1)} %collective-permute-done.3.key_pair.value_pair) | copy-start | bytes 1572868
  38.0 18.0 %copy-start.2 = (bf16[256,1024]{1,0:T(8,128)(2,1)S(1)}, bf16[256,1024]{1,0:T(8,128)(2,1)}, u32[]{:S(2)}) copy-start(bf16[256,1024]{1,0:T(8,128)(2,1)} %get-tuple-element.23) | copy-start | bytes 1572868
  38.0 15.0 %collective-permute-start.8 = (bf16[256,1024]{1,0:T(8,128)(2,1)S(1)}, bf16[256,1024]{1,0:T(8,128)(2,1)}, u32[]{:S(2)}, u32[]{:S(2)}) collective-permute-start(bf16[256,1024]{1,0:T(8,128)(2,1)S(1)} %get-tuple-element.22), channel_id=1, source_target_pairs={{0,16},{16,0},{32,48},{48,32},{1,17},{17,1},{33,49},{49,33},{2,18}... | collective-permute-start | bytes 1572872 | tf_op jit(solution)/shard_map/ppermute | solution.py:224
  38.5 17.5 %collective-permute-start.10 = (bf16[256,1024]{1,0:T(8,128)(2,1)S(1)}, bf16[256,1024]{1,0:T(8,128)(2,1)}, u32[]{:S(2)}, u32[]{:S(2)}) collective-permute-start(bf16[256,1024]{1,0:T(8,128)(2,1)S(1)} %get-tuple-element.24), channel_id=1, source_target_pairs={{0,48},{16,32},{32,16},{48,0},{1,49},{17,33},{33,17},{49,1},{2,50}... | collective-permute-start | bytes 1572872 | tf_op jit(solution)/shard_map/ppermute | solution.py:224
  40.9 16.2 %collective-permute-start = (bf16[2,128,1024]{2,1,0:T(8,128)(2,1)}, bf16[2,128,1024]{2,1,0:T(8,128)(2,1)S(1)}, u32[]{:S(2)}, u32[]{:S(2)}) collective-permute-start(bf16[2,128,1024]{2,1,0:T(8,128)(2,1)} %pad_maximum_fusion), channel_id=1, source_target_pairs={{0,64},{64,0},{1,65},{65,1},{2,66},{66,2},{3,67},{67,3},{4,68},{68... | collective-permute-start | bytes 1572872 | tf_op jit(solution)/shard_map/ppermute | solution.py:200
  40.9 23.2 %collective-permute-start.2 = (bf16[2,128,1024]{2,1,0:T(8,128)(2,1)}, bf16[2,128,1024]{2,1,0:T(8,128)(2,1)S(1)}, u32[]{:S(2)}, u32[]{:S(2)}) collective-permute-start(bf16[2,128,1024]{2,1,0:T(8,128)(2,1)} %collective-permute-done.1.unit_0.unit_1), channel_id=1, source_target_pairs={{0,16},{16,0},{32,48},{48,32},{1,17},{17,1},{33,49},{49,33},{2,18}... | collective-permute-start | bytes 1572872 | tf_op jit(solution)/shard_map/ppermute | solution.py:202
  54.0 25.3 %collective-permute-start.9 = (bf16[128,1024]{1,0:T(8,128)(2,1)S(1)}, bf16[128,1024]{1,0:T(8,128)(2,1)S(1)}, u32[]{:S(2)}, u32[]{:S(2)}) collective-permute-start(bf16[128,1024]{1,0:T(8,128)(2,1)S(1)} %add_convert_fusion.7), channel_id=1, source_target_pairs={{0,48},{16,32},{32,16},{48,0},{1,49},{17,33},{33,17},{49,1},{2,50}... | collective-permute-start | bytes 786440 | tf_op jit(solution)/shard_map/ppermute | solution.py:226
  57.0 23.3 %collective-permute-start.11 = (bf16[128,1024]{1,0:T(8,128)(2,1)S(1)}, bf16[128,1024]{1,0:T(8,128)(2,1)S(1)}, u32[]{:S(2)}, u32[]{:S(2)}) collective-permute-start(bf16[128,1024]{1,0:T(8,128)(2,1)S(1)} %add_convert_fusion.5), channel_id=1, source_target_pairs={{0,16},{16,0},{32,48},{48,32},{1,17},{17,1},{33,49},{49,33},{2,18}... | collective-permute-start | bytes 786440 | tf_op jit(solution)/shard_map/ppermute | solution.py:226
  64.9 15.5 %copy-start.3 = (bf16[256,1024]{1,0:T(8,128)(2,1)S(1)}, bf16[256,1024]{1,0:T(8,128)(2,1)}, u32[]{:S(2)}) copy-start(bf16[256,1024]{1,0:T(8,128)(2,1)} %get-tuple-element.23) | copy-start | bytes 1572868
  77.3 12.7 %collective-permute-start.12 = (bf16[256,1024]{1,0:T(8,128)(2,1)S(1)}, bf16[256,1024]{1,0:T(8,128)(2,1)}, u32[]{:S(2)}, u32[]{:S(2)}) collective-permute-start(bf16[256,1024]{1,0:T(8,128)(2,1)S(1)} %get-tuple-element.26), channel_id=1, source_target_pairs={{0,16},{16,0},{32,48},{48,32},{1,17},{17,1},{33,49},{49,33},{2,18}... | collective-permute-start | bytes 1572872 | tf_op jit(solution)/shard_map/ppermute | solution.py:224
  77.7 15.0 %collective-permute-start.14 = (bf16[256,1024]{1,0:T(8,128)(2,1)S(1)}, bf16[256,1024]{1,0:T(8,128)(2,1)}, u32[]{:S(2)}, u32[]{:S(2)}) collective-permute-start(bf16[256,1024]{1,0:T(8,128)(2,1)S(1)} %get-tuple-element.28), channel_id=1, source_target_pairs={{0,48},{16,32},{32,16},{48,0},{1,49},{17,33},{33,17},{49,1},{2,50}... | collective-permute-start | bytes 1572872 | tf_op jit(solution)/shard_map/ppermute | solution.py:224
  82.3 19.9 %all-to-all-start = ((bf16[16,2,8,1024]{3,2,1,0:T(8,128)(2,1)}), bf16[16,2,8,1024]{3,2,1,0:T(8,128)(2,1)S(1)}, u32[]{:S(2)}, u32[]{:S(2)}) async-start(bf16[16,2,8,1024]{3,2,1,0:T(8,128)(2,1)} %pad_maximum_fusion.3), calls=%async_computation | async-start | bytes 1048576 | tf_op jit(solution)/shard_map/all_to_all | solution.py:233
  91.0 7.7 %collective-permute-start.13 = (bf16[128,1024]{1,0:T(8,128)(2,1)S(1)}, bf16[128,1024]{1,0:T(8,128)(2,1)S(1)}, u32[]{:S(2)}, u32[]{:S(2)}) collective-permute-start(bf16[128,1024]{1,0:T(8,128)(2,1)S(1)} %add_convert_fusion.3), channel_id=1, source_target_pairs={{0,48},{16,32},{32,16},{48,0},{1,49},{17,33},{33,17},{49,1},{2,50}... | collective-permute-start | bytes 786440 | tf_op jit(solution)/shard_map/ppermute | solution.py:226
  93.8 6.5 %collective-permute-start.15 = (bf16[128,1024]{1,0:T(8,128)(2,1)S(1)}, bf16[128,1024]{1,0:T(8,128)(2,1)S(1)}, u32[]{:S(2)}, u32[]{:S(2)}) collective-permute-start(bf16[128,1024]{1,0:T(8,128)(2,1)S(1)} %add_convert_fusion.1), channel_id=1, source_target_pairs={{0,16},{16,0},{32,48},{48,32},{1,17},{17,1},{33,49},{49,33},{2,18}... | collective-permute-start | bytes 786440 | tf_op jit(solution)/shard_map/ppermute | solution.py:226
  102.2 19.6 %all-to-all-start.1 = ((bf16[16,2,8,1024]{3,2,1,0:T(8,128)(2,1)}), bf16[16,2,8,1024]{3,2,1,0:T(8,128)(2,1)S(1)}, u32[]{:S(2)}, u32[]{:S(2)}) async-start(bf16[16,2,8,1024]{3,2,1,0:T(8,128)(2,1)} %pad_maximum_fusion.4), calls=%async_computation.1 | async-start | bytes 1048576 | tf_op jit(solution)/shard_map/all_to_all | solution.py:233
  (1 other events, 0.8 us)

commit v5 on v3

--- a/solution.py
+++ b/solution.py
@@ -129,7 +129,7 @@
         grid_spec=grid_spec,
         out_shape=[jax.ShapeDtypeStruct(query.shape, jnp.bfloat16)] + [grads] * 4,
         input_output_aliases={14: 0} if buffer else {},
-        compiler_params=pltpu.CompilerParams(dimension_semantics=("arbitrary",), vmem_limit_bytes=48 * 2**20),
+        compiler_params=pltpu.CompilerParams(dimension_semantics=("arbitrary",), vmem_limit_bytes=49 * 2**20),
         cost_estimate=pl.CostEstimate(
             flops=5 * count * matmul, transcendentals=count * tokens * 512, bytes_accessed=count * 2**20
         ),
@@ -182,12 +182,13 @@
 
     gathered = []
     first = 0
-    for counts in GATHERS:
+    for n, counts in enumerate(GATHERS):
         at, width = first * HEAD, sum(counts) * HEAD
-        sent = jnp.where(
-            wants_values, columns(values, there * local + at, width), columns(keys, there * local + at, width)
-        )
-        pair = jnp.stack([columns(a, pair_owner * local + at, width) for a in (keys, values)])
+        sent = [columns(a, there * local + at, width) for a in (keys, values)]
+        sent = jnp.where(wants_values, sent[1], sent[0])
+        if n == 0:
+            keys_too, values_too, sent = lax.optimization_barrier((keys, values, sent))
+        pair = jnp.stack([columns(a, pair_owner * local + at, width) for a in (keys_too, values_too)])
         unit = lax.ppermute(sent, ("yh", "c", "x", "yl"), to_cross)
         pair = lax.ppermute(pair, "c", [(0, 1), (1, 0)])
         units = [unit]

time: 119 us -> 118 us (level)
  waiting for transfers between devices: 50.2 us -> 47.1 us
  local copies, waits for them, and re-layouts: 0.13 us -> 1.37 us
    select_n x1, other arithmetic: 2.76 us -> 1.39 us  [shards(): sent = jnp.where(wants_values, sent[1], sent[0])]
    all_to_all x2, waiting for transfers between devices: 14.8 us -> 13.4 us  [shards(): lax.all_to_all(both, ('yl', 'z'), split_axis=0, concat_axis=0, tiled=True)]
    another operation x0 -> x1, local copies, waits for them, and re-layouts: none -> 1.26 us  [shards(): jnp.stack([columns(a, pair_owner * local + at, width) for a in (keys_too,...]
  transfers between devices with their start and end apart: 20 -> 20, of which waited for: 14 -> 13; matrix products, arithmetic and copies ran while one was open for 3% -> 5% of each run, Pallas kernels for 10% -> 10%
where the time goes in v5:
time: 118 us; the launch traced here: 116 us
  waiting for transfers between devices  47.1 us (40%)
  starting transfers between devices  35.8 us (30%)
  Pallas kernels  24.4 us (21%)
  other arithmetic  6.67 us (6%)
  local copies, waits for them, and re-layouts  1.37 us (1%)
    pallas_call x2, Pallas kernels, attention(): pl.pallas_call(functools.partial(attention_body, first=first, scale=SCALE...  24.4 us
    ppermute x6, waiting for transfers between devices, shards(): lax.ppermute(unit, axis, [(i, (i + by) % size) for i in range(size)])  15.5 us
    all_to_all x2, waiting for transfers between devices, shards(): lax.all_to_all(both, ('yl', 'z'), split_axis=0, concat_axis=0, tiled=True)  13.4 us
    all_to_all x2, starting transfers between devices, shards(): lax.all_to_all(both, ('yl', 'z'), split_axis=0, concat_axis=0, tiled=True)  11.3 us
    ppermute x2, waiting for transfers between devices, shards(): unit = lax.ppermute(sent, ('yh', 'c', 'x', 'yl'), to_cross)  10.5 us
    ppermute x4, starting transfers between devices, shards(): passed = lax.ppermute(passed, 'x', far)  6.81 us
    ppermute x6, starting transfers between devices, shards(): lax.ppermute(unit, axis, [(i, (i + by) % size) for i in range(size)])  5.97 us
    ppermute x4, starting transfers between devices, shards(): got = lax.ppermute(send, 'x', near)  4.95 us
  transfers between devices with their start and end apart: 20, of which 13 were waited for; matrix products, arithmetic and copies ran while one was open for 5% of the time, Pallas kernels for 10%

profile of v5, /device:TPU:2, one launch (start us, length us, event | category | flops | bytes accessed | tf_op | source)
XLA Modules:
  0.0 116.2 jit_solution(10016469391261433914)
XLA Ops:
  0.7 1.4 %select_bitcast_fusion = (bf16[128,1024]{1,0:T(8,128)(2,1)S(1)}, bf16[128,1024]{1,0:T(8,128)(2,1)S(1)}) fusion(bf16[1,128,8192]{2,1,0:T(8,128)(2,1)} %param.8, s32[]{:T(128)S(6)} %select_n.105, bf16[1,128,8192]{2,1,0:T(8,128)(2,1)} %param.9, pred[]{:T(512)S(6)} %eq.13, s32[]{:T(128)S(6)} %select_n.101), kind=kLoop, calls=%fused_computation.20 | loop fusion | flops 262144 | bytes 1572873 | tf_op jit(solution)/shard_map/jit(_where)/select_n | solution.py:188
  2.1 2.5 %collective-permute-start.6 = (bf16[128,1024]{1,0:T(8,128)(2,1)S(1)}, bf16[128,1024]{1,0:T(8,128)(2,1)S(1)}, u32[]{:S(2)}, u32[]{:S(2)}) collective-permute-start(bf16[128,1024]{1,0:T(8,128)(2,1)S(1)} %get-tuple-element.18), channel_id=1, source_target_pairs={{0,136},{8,128},{16,216},{24,208},{32,168},{40,160},{48,248},{56,2... | collective-permute-start | bytes 786440 | tf_op jit(solution)/shard_map/ppermute | solution.py:192
  6.7 4.9 %collective-permute-done.6.unit_0 = bf16[128,1024]{1,0:T(8,128)(2,1)S(1)} collective-permute-done((bf16[128,1024]{1,0:T(8,128)(2,1)S(1)}, bf16[128,1024]{1,0:T(8,128)(2,1)S(1)}, u32[]{:S(2)}, u32[]{:S(2)}) %collective-permute-start.6) | collective-permute-done | bytes 262176 | tf_op jit(solution)/shard_map/ppermute | solution.py:192
  11.7 1.4 %collective-permute-start.7 = (bf16[128,1024]{1,0:T(8,128)(2,1)S(1)}, bf16[128,1024]{1,0:T(8,128)(2,1)S(1)}, u32[]{:S(2)}, u32[]{:S(2)}) collective-permute-start(bf16[128,1024]{1,0:T(8,128)(2,1)S(1)} %collective-permute-done.6.unit_0), channel_id=1, source_target_pairs={{0,16},{16,32},{32,48},{48,0},{1,17},{17,33},{33,49},{49,1},{2,18}... | collective-permute-start | bytes 786440 | tf_op jit(solution)/shard_map/ppermute | solution.py:196
  13.7 1.9 %collective-permute-start.9 = (bf16[128,1024]{1,0:T(8,128)(2,1)S(1)}, bf16[128,1024]{1,0:T(8,128)(2,1)S(1)}, u32[]{:S(2)}, u32[]{:S(2)}) collective-permute-start(bf16[128,1024]{1,0:T(8,128)(2,1)S(1)} %collective-permute-done.6.unit_0), channel_id=1, source_target_pairs={{0,1},{1,2},{2,3},{3,4},{4,5},{5,6},{6,7},{7,0},{8,9},{9,10},{10,1... | collective-permute-start | bytes 786440 | tf_op jit(solution)/shard_map/ppermute | solution.py:196
  15.7 4.3 %collective-permute-done.7.unit_1 = bf16[128,1024]{1,0:T(8,128)(2,1)S(1)} collective-permute-done((bf16[128,1024]{1,0:T(8,128)(2,1)S(1)}, bf16[128,1024]{1,0:T(8,128)(2,1)S(1)}, u32[]{:S(2)}, u32[]{:S(2)}) %collective-permute-start.7) | collective-permute-done | bytes 262176 | tf_op jit(solution)/shard_map/ppermute | solution.py:196
  20.7 4.9 %collective-permute-done.9.unit_3 = bf16[128,1024]{1,0:T(8,128)(2,1)S(1)} collective-permute-done((bf16[128,1024]{1,0:T(8,128)(2,1)S(1)}, bf16[128,1024]{1,0:T(8,128)(2,1)S(1)}, u32[]{:S(2)}, u32[]{:S(2)}) %collective-permute-start.9) | collective-permute-done | bytes 262176 | tf_op jit(solution)/shard_map/ppermute | solution.py:196
  25.6 12.2 %attention.2 = (bf16[640,2048]{1,0:T(8,128)(2,1)}, bf16[256,1024]{1,0:T(8,128)(2,1)S(1)}, bf16[256,1024]{1,0:T(8,128)(2,1)S(1)}, bf16[256,1024]{1,0:T(8,128)(2,1)S(1)}, bf16[256,1024]{1,0:T(8,128)(2,1)S(1)}) custom-call(s32[17]{0:T(128)S(1)} %stack.95.place, s32[8]{0:T(128)S(1)} %bitcast.53, f32[16]{0:T(128)S(1)} %tanh_bitcast_fusion.factor, ...), custom_call_target="tpu_custom_call" | custom-call | flops 3355443200 | bytes 8388608 | tf_op jit(solution)/shard_map/attention/pallas_call | solution.py:127
  37.8 1.5 %collective-permute-start.10 = (bf16[256,1024]{1,0:T(8,128)(2,1)S(1)}, bf16[256,1024]{1,0:T(8,128)(2,1)S(1)}, u32[]{:S(2)}, u32[]{:S(2)}) collective-permute-start(bf16[256,1024]{1,0:T(8,128)(2,1)S(1)} %get-tuple-element.22), channel_id=1, source_target_pairs={{0,16},{16,0},{32,48},{48,32},{1,17},{17,1},{33,49},{49,33},{2,18}... | collective-permute-start | bytes 1572872 | tf_op jit(solution)/shard_map/ppermute | solution.py:216
  40.5 1.3 %collective-permute-start.1 = (bf16[128,1024]{1,0:T(8,128)(2,1)S(1)}, bf16[128,1024]{1,0:T(8,128)(2,1)S(1)}, u32[]{:S(2)}, u32[]{:S(2)}) collective-permute-start(bf16[128,1024]{1,0:T(8,128)(2,1)S(1)} %get-tuple-element.29), channel_id=1, source_target_pairs={{0,136},{8,128},{16,216},{24,208},{32,168},{40,160},{48,248},{56,2... | collective-permute-start | bytes 786440 | tf_op jit(solution)/shard_map/ppermute | solution.py:192
  41.9 2.2 %collective-permute-start = (bf16[2,128,1024]{2,1,0:T(8,128)(2,1)S(1)}, bf16[2,128,1024]{2,1,0:T(8,128)(2,1)S(1)}, u32[]{:S(2)}, u32[]{:S(2)}) collective-permute-start(bf16[2,128,1024]{2,1,0:T(8,128)(2,1)S(1)} %pad_maximum_fusion), channel_id=1, source_target_pairs={{0,64},{64,0},{1,65},{65,1},{2,66},{66,2},{3,67},{67,3},{4,68},{68... | collective-permute-start | bytes 1572872 | tf_op jit(solution)/shard_map/ppermute | solution.py:193
  44.1 5.6 %collective-permute-done.1.unit_0 = bf16[128,1024]{1,0:T(8,128)(2,1)S(1)} collective-permute-done((bf16[128,1024]{1,0:T(8,128)(2,1)S(1)}, bf16[128,1024]{1,0:T(8,128)(2,1)S(1)}, u32[]{:S(2)}, u32[]{:S(2)}) %collective-permute-start.1) | collective-permute-done | bytes 262176 | tf_op jit(solution)/shard_map/ppermute | solution.py:192
  49.9 1.9 %collective-permute-start.3 = (bf16[128,1024]{1,0:T(8,128)(2,1)S(1)}, bf16[128,1024]{1,0:T(8,128)(2,1)S(1)}, u32[]{:S(2)}, u32[]{:S(2)}) collective-permute-start(bf16[128,1024]{1,0:T(8,128)(2,1)S(1)} %collective-permute-done.1.unit_0), channel_id=1, source_target_pairs={{0,48},{16,0},{32,16},{48,32},{1,49},{17,1},{33,17},{49,33},{2,50}... | collective-permute-start | bytes 786440 | tf_op jit(solution)/shard_map/ppermute | solution.py:196
  51.9 1.3 %collective-permute-start.11 = (bf16[128,1024]{1,0:T(8,128)(2,1)S(1)}, bf16[128,1024]{1,0:T(8,128)(2,1)S(1)}, u32[]{:S(2)}, u32[]{:S(2)}) collective-permute-start(bf16[128,1024]{1,0:T(8,128)(2,1)S(1)} %add_convert_fusion.7), channel_id=1, source_target_pairs={{0,48},{16,32},{32,16},{48,0},{1,49},{17,33},{33,17},{49,1},{2,50}... | collective-permute-start | bytes 786440 | tf_op jit(solution)/shard_map/ppermute | solution.py:218
  53.3 2.2 %collective-permute-start.13 = (bf16[128,1024]{1,0:T(8,128)(2,1)S(1)}, bf16[128,1024]{1,0:T(8,128)(2,1)S(1)}, u32[]{:S(2)}, u32[]{:S(2)}) collective-permute-start(bf16[128,1024]{1,0:T(8,128)(2,1)S(1)} %add_convert_fusion.5), channel_id=1, source_target_pairs={{0,16},{16,0},{32,48},{48,32},{1,17},{17,1},{33,49},{49,33},{2,18}... | collective-permute-start | bytes 786440 | tf_op jit(solution)/shard_map/ppermute | solution.py:218
  55.4 3.4 %collective-permute-done.2.unit_1 = bf16[128,1024]{1,0:T(8,128)(2,1)S(1)} collective-permute-done((bf16[128,1024]{1,0:T(8,128)(2,1)S(1)}, bf16[128,1024]{1,0:T(8,128)(2,1)S(1)}, u32[]{:S(2)}, u32[]{:S(2)}) %collective-permute-start.2) | collective-permute-done | bytes 262176 | tf_op jit(solution)/shard_map/ppermute | solution.py:196
  59.0 2.0 %collective-permute-done.4.unit_3 = bf16[128,1024]{1,0:T(8,128)(2,1)S(1)} collective-permute-done((bf16[128,1024]{1,0:T(8,128)(2,1)S(1)}, bf16[128,1024]{1,0:T(8,128)(2,1)S(1)}, u32[]{:S(2)}, u32[]{:S(2)}) %collective-permute-start.4) | collective-permute-done | bytes 262176 | tf_op jit(solution)/shard_map/ppermute | solution.py:196
  61.0 12.2 %attention.3 = (bf16[640,2048]{1,0:T(8,128)(2,1)}, bf16[256,1024]{1,0:T(8,128)(2,1)S(1)}, bf16[256,1024]{1,0:T(8,128)(2,1)S(1)}, bf16[256,1024]{1,0:T(8,128)(2,1)S(1)}, bf16[256,1024]{1,0:T(8,128)(2,1)S(1)}) custom-call(s32[17]{0:T(128)S(1)} %stack.95.place, s32[8]{0:T(128)S(1)} %bitcast.54, ...), custom_call_target="tpu_custom_call", output_to_operand_aliasing={{0}: (14, {})} | custom-call | flops 3355443200 | bytes 8388608 | tf_op jit(solution)/shard_map/attention/pallas_call | solution.py:127
  76.6 5.7 %all-to-all-start = ((bf16[16,2,8,1024]{3,2,1,0:T(8,128)(2,1)}), bf16[16,2,8,1024]{3,2,1,0:T(8,128)(2,1)S(1)}, u32[]{:S(2)}, u32[]{:S(2)}) async-start(bf16[16,2,8,1024]{3,2,1,0:T(8,128)(2,1)} %pad_maximum_fusion.2), calls=%async_computation | async-start | bytes 1048576 | tf_op jit(solution)/shard_map/all_to_all | solution.py:225
  82.3 3.9 %collective-permute-done.14 = bf16[256,1024]{1,0:T(8,128)(2,1)} collective-permute-done((bf16[256,1024]{1,0:T(8,128)(2,1)S(1)}, bf16[256,1024]{1,0:T(8,128)(2,1)}, u32[]{:S(2)}, u32[]{:S(2)}) %collective-permute-start.14) | collective-permute-done | bytes 524320 | tf_op jit(solution)/shard_map/ppermute | solution.py:216
  88.3 2.4 %collective-permute-start.17 = (bf16[128,1024]{1,0:T(8,128)(2,1)S(1)}, bf16[128,1024]{1,0:T(8,128)(2,1)S(1)}, u32[]{:S(2)}, u32[]{:S(2)}) collective-permute-start(bf16[128,1024]{1,0:T(8,128)(2,1)S(1)} %add_convert_fusion.1), channel_id=1, source_target_pairs={{0,16},{16,0},{32,48},{48,32},{1,17},{17,1},{33,49},{49,33},{2,18}... | collective-permute-start | bytes 786440 | tf_op jit(solution)/shard_map/ppermute | solution.py:218
  90.6 3.1 %collective-permute-done.15 = bf16[128,1024]{1,0:T(8,128)(2,1)S(1)} collective-permute-done((bf16[128,1024]{1,0:T(8,128)(2,1)S(1)}, bf16[128,1024]{1,0:T(8,128)(2,1)S(1)}, u32[]{:S(2)}, u32[]{:S(2)}) %collective-permute-start.15) | collective-permute-done | bytes 262176 | tf_op jit(solution)/shard_map/ppermute | solution.py:218
  96.3 5.6 %all-to-all-start.1 = ((bf16[16,2,8,1024]{3,2,1,0:T(8,128)(2,1)}), bf16[16,2,8,1024]{3,2,1,0:T(8,128)(2,1)S(1)}, u32[]{:S(2)}, u32[]{:S(2)}) async-start(bf16[16,2,8,1024]{3,2,1,0:T(8,128)(2,1)} %pad_maximum_fusion.3), calls=%async_computation.1 | async-start | bytes 1048576 | tf_op jit(solution)/shard_map/all_to_all | solution.py:225
  102.0 13.4 %all-to-all-done.1 = bf16[16,2,8,1024]{3,2,1,0:T(8,128)(2,1)S(1)} async-done(((bf16[16,2,8,1024]{3,2,1,0:T(8,128)(2,1)}), bf16[16,2,8,1024]{3,2,1,0:T(8,128)(2,1)S(1)}, u32[]{:S(2)}, u32[]{:S(2)}) %all-to-all-start.1) | async-done | bytes 524320 | tf_op jit(solution)/shard_map/all_to_all | solution.py:225
  (44 shorter events, 14.2 us)
Async XLA Ops:
  2.1 13.5 %copy-start.1 = (s32[640]{0:T(1024)S(1)}, s32[640]{0:T(1024)}, u32[]{:S(2)}) copy-start(s32[640]{0:T(1024)} %param.13) | copy-start | bytes 7684
  2.1 13.6 %copy-start.2 = (f32[1,16]{1,0:T(1,128)S(1)}, f32[1,16]{1,0:T(1,128)}, u32[]{:S(2)}) copy-start(f32[1,16]{1,0:T(1,128)} %param.11) | copy-start | bytes 196
  2.1 23.5 %copy-start = (s32[1,8]{1,0:T(1,128)S(1)}, s32[1,8]{1,0:T(1,128)}, u32[]{:S(2)}) copy-start(s32[1,8]{1,0:T(1,128)} %param.12) | copy-start | bytes 100
  2.1 9.5 %collective-permute-start.6 = (bf16[128,1024]{1,0:T(8,128)(2,1)S(1)}, bf16[128,1024]{1,0:T(8,128)(2,1)S(1)}, u32[]{:S(2)}, u32[]{:S(2)}) collective-permute-start(bf16[128,1024]{1,0:T(8,128)(2,1)S(1)} %get-tuple-element.18), channel_id=1, source_target_pairs={{0,136},{8,128},{16,216},{24,208},{32,168},{40,160},{48,248},{56,2... | collective-permute-start | bytes 786440 | tf_op jit(solution)/shard_map/ppermute | solution.py:192
  6.0 9.7 %collective-permute-start.5 = (bf16[2,128,1024]{2,1,0:T(8,128)(2,1)S(1)}, bf16[2,128,1024]{2,1,0:T(8,128)(2,1)S(1)}, u32[]{:S(2)}, u32[]{:S(2)}) collective-permute-start(bf16[2,128,1024]{2,1,0:T(8,128)(2,1)S(1)} %pad_maximum_fusion.1), channel_id=1, source_target_pairs={{0,64},{64,0},{1,65},{65,1},{2,66},{66,2},{3,67},{67,3},{4,68},{68... | collective-permute-start | bytes 1572872 | tf_op jit(solution)/shard_map/ppermute | solution.py:193
  11.7 8.4 %collective-permute-start.7 = (bf16[128,1024]{1,0:T(8,128)(2,1)S(1)}, bf16[128,1024]{1,0:T(8,128)(2,1)S(1)}, u32[]{:S(2)}, u32[]{:S(2)}) collective-permute-start(bf16[128,1024]{1,0:T(8,128)(2,1)S(1)} %collective-permute-done.6.unit_0), channel_id=1, source_target_pairs={{0,16},{16,32},{32,48},{48,0},{1,17},{17,33},{33,49},{49,1},{2,18}... | collective-permute-start | bytes 786440 | tf_op jit(solution)/shard_map/ppermute | solution.py:196
  13.0 7.7 %collective-permute-start.8 = (bf16[128,1024]{1,0:T(8,128)(2,1)S(1)}, bf16[128,1024]{1,0:T(8,128)(2,1)S(1)}, u32[]{:S(2)}, u32[]{:S(2)}) collective-permute-start(bf16[128,1024]{1,0:T(8,128)(2,1)S(1)} %collective-permute-done.6.unit_0), channel_id=1, source_target_pairs={{0,48},{16,0},{32,16},{48,32},{1,49},{17,1},{33,17},{49,33},{2,50}... | collective-permute-start | bytes 786440 | tf_op jit(solution)/shard_map/ppermute | solution.py:196
  13.7 11.9 %collective-permute-start.9 = (bf16[128,1024]{1,0:T(8,128)(2,1)S(1)}, bf16[128,1024]{1,0:T(8,128)(2,1)S(1)}, u32[]{:S(2)}, u32[]{:S(2)}) collective-permute-start(bf16[128,1024]{1,0:T(8,128)(2,1)S(1)} %collective-permute-done.6.unit_0), channel_id=1, source_target_pairs={{0,1},{1,2},{2,3},{3,4},{4,5},{5,6},{6,7},{7,0},{8,9},{9,10},{10,1... | collective-permute-start | bytes 786440 | tf_op jit(solution)/shard_map/ppermute | solution.py:196
  37.8 13.9 %collective-permute-start.10 = (bf16[256,1024]{1,0:T(8,128)(2,1)S(1)}, bf16[256,1024]{1,0:T(8,128)(2,1)S(1)}, u32[]{:S(2)}, u32[]{:S(2)}) collective-permute-start(bf16[256,1024]{1,0:T(8,128)(2,1)S(1)} %get-tuple-element.22), channel_id=1, source_target_pairs={{0,16},{16,0},{32,48},{48,32},{1,17},{17,1},{33,49},{49,33},{2,18}... | collective-permute-start | bytes 1572872 | tf_op jit(solution)/shard_map/ppermute | solution.py:216
  39.4 12.5 %collective-permute-start.12 = (bf16[256,1024]{1,0:T(8,128)(2,1)S(1)}, bf16[256,1024]{1,0:T(8,128)(2,1)S(1)}, u32[]{:S(2)}, u32[]{:S(2)}) collective-permute-start(bf16[256,1024]{1,0:T(8,128)(2,1)S(1)} %get-tuple-element.24), channel_id=1, source_target_pairs={{0,48},{16,32},{32,16},{48,0},{1,49},{17,33},{33,17},{49,1},{2,50}... | collective-permute-start | bytes 1572872 | tf_op jit(solution)/shard_map/ppermute | solution.py:216
  40.5 9.2 %collective-permute-start.1 = (bf16[128,1024]{1,0:T(8,128)(2,1)S(1)}, bf16[128,1024]{1,0:T(8,128)(2,1)S(1)}, u32[]{:S(2)}, u32[]{:S(2)}) collective-permute-start(bf16[128,1024]{1,0:T(8,128)(2,1)S(1)} %get-tuple-element.29), channel_id=1, source_target_pairs={{0,136},{8,128},{16,216},{24,208},{32,168},{40,160},{48,248},{56,2... | collective-permute-start | bytes 786440 | tf_op jit(solution)/shard_map/ppermute | solution.py:192
  41.9 11.4 %collective-permute-start = (bf16[2,128,1024]{2,1,0:T(8,128)(2,1)S(1)}, bf16[2,128,1024]{2,1,0:T(8,128)(2,1)S(1)}, u32[]{:S(2)}, u32[]{:S(2)}) collective-permute-start(bf16[2,128,1024]{2,1,0:T(8,128)(2,1)S(1)} %pad_maximum_fusion), channel_id=1, source_target_pairs={{0,64},{64,0},{1,65},{65,1},{2,66},{66,2},{3,67},{67,3},{4,68},{68... | collective-permute-start | bytes 1572872 | tf_op jit(solution)/shard_map/ppermute | solution.py:193
  49.7 9.2 %collective-permute-start.2 = (bf16[128,1024]{1,0:T(8,128)(2,1)S(1)}, bf16[128,1024]{1,0:T(8,128)(2,1)S(1)}, u32[]{:S(2)}, u32[]{:S(2)}) collective-permute-start(bf16[128,1024]{1,0:T(8,128)(2,1)S(1)} %collective-permute-done.1.unit_0), channel_id=1, source_target_pairs={{0,16},{16,32},{32,48},{48,0},{1,17},{17,33},{33,49},{49,1},{2,18}... | collective-permute-start | bytes 786440 | tf_op jit(solution)/shard_map/ppermute | solution.py:196
  49.9 9.2 %collective-permute-start.3 = (bf16[128,1024]{1,0:T(8,128)(2,1)S(1)}, bf16[128,1024]{1,0:T(8,128)(2,1)S(1)}, u32[]{:S(2)}, u32[]{:S(2)}) collective-permute-start(bf16[128,1024]{1,0:T(8,128)(2,1)S(1)} %collective-permute-done.1.unit_0), channel_id=1, source_target_pairs={{0,48},{16,0},{32,16},{48,32},{1,49},{17,1},{33,17},{49,33},{2,50}... | collective-permute-start | bytes 786440 | tf_op jit(solution)/shard_map/ppermute | solution.py:196
  51.7 9.3 %collective-permute-start.4 = (bf16[128,1024]{1,0:T(8,128)(2,1)S(1)}, bf16[128,1024]{1,0:T(8,128)(2,1)S(1)}, u32[]{:S(2)}, u32[]{:S(2)}) collective-permute-start(bf16[128,1024]{1,0:T(8,128)(2,1)S(1)} %collective-permute-done.1.unit_0), channel_id=1, source_target_pairs={{0,1},{1,2},{2,3},{3,4},{4,5},{5,6},{6,7},{7,0},{8,9},{9,10},{10,1... | collective-permute-start | bytes 786440 | tf_op jit(solution)/shard_map/ppermute | solution.py:196
  51.9 23.6 %collective-permute-start.11 = (bf16[128,1024]{1,0:T(8,128)(2,1)S(1)}, bf16[128,1024]{1,0:T(8,128)(2,1)S(1)}, u32[]{:S(2)}, u32[]{:S(2)}) collective-permute-start(bf16[128,1024]{1,0:T(8,128)(2,1)S(1)} %add_convert_fusion.7), channel_id=1, source_target_pairs={{0,48},{16,32},{32,16},{48,0},{1,49},{17,33},{33,17},{49,1},{2,50}... | collective-permute-start | bytes 786440 | tf_op jit(solution)/shard_map/ppermute | solution.py:218
  53.3 22.4 %collective-permute-start.13 = (bf16[128,1024]{1,0:T(8,128)(2,1)S(1)}, bf16[128,1024]{1,0:T(8,128)(2,1)S(1)}, u32[]{:S(2)}, u32[]{:S(2)}) collective-permute-start(bf16[128,1024]{1,0:T(8,128)(2,1)S(1)} %add_convert_fusion.5), channel_id=1, source_target_pairs={{0,16},{16,0},{32,48},{48,32},{1,17},{17,1},{33,49},{49,33},{2,18}... | collective-permute-start | bytes 786440 | tf_op jit(solution)/shard_map/ppermute | solution.py:218
  73.2 13.0 %collective-permute-start.14 = (bf16[256,1024]{1,0:T(8,128)(2,1)S(1)}, bf16[256,1024]{1,0:T(8,128)(2,1)}, u32[]{:S(2)}, u32[]{:S(2)}) collective-permute-start(bf16[256,1024]{1,0:T(8,128)(2,1)S(1)} %get-tuple-element.26), channel_id=1, source_target_pairs={{0,16},{16,0},{32,48},{48,32},{1,17},{17,1},{33,49},{49,33},{2,18}... | collective-permute-start | bytes 1572872 | tf_op jit(solution)/shard_map/ppermute | solution.py:216
  74.4 13.8 %collective-permute-start.16 = (bf16[256,1024]{1,0:T(8,128)(2,1)S(1)}, bf16[256,1024]{1,0:T(8,128)(2,1)S(1)}, u32[]{:S(2)}, u32[]{:S(2)}) collective-permute-start(bf16[256,1024]{1,0:T(8,128)(2,1)S(1)} %get-tuple-element.28), channel_id=1, source_target_pairs={{0,48},{16,32},{32,16},{48,0},{1,49},{17,33},{33,17},{49,1},{2,50}... | collective-permute-start | bytes 1572872 | tf_op jit(solution)/shard_map/ppermute | solution.py:216
  76.6 19.7 %all-to-all-start = ((bf16[16,2,8,1024]{3,2,1,0:T(8,128)(2,1)}), bf16[16,2,8,1024]{3,2,1,0:T(8,128)(2,1)S(1)}, u32[]{:S(2)}, u32[]{:S(2)}) async-start(bf16[16,2,8,1024]{3,2,1,0:T(8,128)(2,1)} %pad_maximum_fusion.2), calls=%async_computation | async-start | bytes 1048576 | tf_op jit(solution)/shard_map/all_to_all | solution.py:225
  87.2 6.5 %collective-permute-start.15 = (bf16[128,1024]{1,0:T(8,128)(2,1)S(1)}, bf16[128,1024]{1,0:T(8,128)(2,1)S(1)}, u32[]{:S(2)}, u32[]{:S(2)}) collective-permute-start(bf16[128,1024]{1,0:T(8,128)(2,1)S(1)} %add_convert_fusion.3), channel_id=1, source_target_pairs={{0,48},{16,32},{32,16},{48,0},{1,49},{17,33},{33,17},{49,1},{2,50}... | collective-permute-start | bytes 786440 | tf_op jit(solution)/shard_map/ppermute | solution.py:218
  88.3 7.0 %collective-permute-start.17 = (bf16[128,1024]{1,0:T(8,128)(2,1)S(1)}, bf16[128,1024]{1,0:T(8,128)(2,1)S(1)}, u32[]{:S(2)}, u32[]{:S(2)}) collective-permute-start(bf16[128,1024]{1,0:T(8,128)(2,1)S(1)} %add_convert_fusion.1), channel_id=1, source_target_pairs={{0,16},{16,0},{32,48},{48,32},{1,17},{17,1},{33,49},{49,33},{2,18}... | collective-permute-start | bytes 786440 | tf_op jit(solution)/shard_map/ppermute | solution.py:218
  96.3 19.1 %all-to-all-start.1 = ((bf16[16,2,8,1024]{3,2,1,0:T(8,128)(2,1)}), bf16[16,2,8,1024]{3,2,1,0:T(8,128)(2,1)S(1)}, u32[]{:S(2)}, u32[]{:S(2)}) async-start(bf16[16,2,8,1024]{3,2,1,0:T(8,128)(2,1)} %pad_maximum_fusion.3), calls=%async_computation.1 | async-start | bytes 1048576 | tf_op jit(solution)/shard_map/all_to_all | solution.py:225
